TPU v7x, 256 devices: a whole 4x4x8 slice. The times are simulated.
256 devices in a mesh: dp: 32 (over z_hi, y, core), level: 8 (over x, z_lo).
Axes of the slice: x: 4, y: 4, z: 8 (z_hi: 4, z_lo: 2; z = z_hi * 2 + z_lo), core: 2. Of those that a mesh axis runs over, the one named last changes fastest.
Arguments:
- token_ids: int32 [32, 8, 1536], P('dp', 'level'), may hold values from 0 to 1023
- decoded_mask: int32 [32, 8, 1536], P('dp', 'level'), may hold values 0 or 1
- levels_done: int32 [32], P('dp'), may hold values from 0 to 7
- code_tables: bfloat16 [8, 1024, 1024], P('level'), may hold values from -6 to 6
- mask_vectors: bfloat16 [8, 1024], P('level'), may hold values from -6 to 6
- w_qkv: bfloat16 [3, 1024, 1024], P(None, 'dp', 'level'), may hold values from -6 to 6
- w_out: bfloat16 [1024, 1024], P('level', 'dp'), may hold values from -0.1875 to 0.1875
- w_expand: bfloat16 [1024, 2048], P('dp'), may hold values from -0.1875 to 0.1875
- w_depth: bfloat16 [5, 1024], replicated, may hold values from -2.5 to 2.5
- w_project: bfloat16 [1024, 1024], P('dp'), may hold values from -0.1875 to 0.1875
- level_heads: bfloat16 [8, 1024, 1024], P('level'), may hold values from -0.1875 to 0.1875
Outputs:
- logits: bfloat16 [32, 8, 1536, 1024], P('dp', 'level')
Inputs may be any that keep to these rules, and one draw needn't show every extreme that they name: `levels_done`: levels below it are fully decoded; the level equal to it is the one being decoded.
All inputs are finite; a program needn't handle non-finite values. No bound on the sum of `decoded_mask` on one device may be relied on, other than what follows from the above.
Results may differ from a plain program's by a relative error of at most 0.006.
Values may be sent and summed in bfloat16 or wider, within the bound.
A program may use at most 128 MiB of HBM per device.

v0:
```python
import jax
import jax.numpy as jnp
from jax import lax
from jax.sharding import PartitionSpec as P

HEADS = 16


def copy_for_each(x, axis):
    copies = jnp.broadcast_to(x, (lax.axis_size(axis), *x.shape))
    return lax.all_to_all(copies, axis, split_axis=0, concat_axis=0, tiled=True)


def laid_out(tiles, dim):
    tiles = jnp.moveaxis(tiles, 0, dim)
    dims = tiles.shape
    return tiles.reshape(*dims[:dim], dims[dim] * dims[dim + 1], *dims[dim + 2 :])


def gather_directly(x, axis, dim):
    tiles = copy_for_each(x, axis)
    return laid_out(tiles, dim)


def side_by_side(arrays, axis, dim, along):
    ends, at = ([], 0)
    for a in arrays[:-1]:
        at += a.shape[along]
        ends.append(at)
    both = jnp.concatenate(arrays, axis=along)
    return tuple(jnp.split(lax.all_gather(both, axis, axis=dim, tiled=True), ends, axis=along))


def with_halo(x, sides, width):
    for axis, dim in sides:
        devices, length = (lax.axis_size(axis), x.shape[dim])
        up = [(i, (i + 1) % devices) for i in range(devices - 1)]
        down = [(j, i) for i, j in up]
        last = lax.slice_in_dim(x, length - width, length, axis=dim)
        leading = lax.slice_in_dim(x, 0, width, axis=dim)
        before = lax.ppermute(last, axis, up)
        after = lax.ppermute(leading, axis, down)
        x = jnp.concatenate([before, x, after], axis=dim)
    return x


def layer_norm(values):
    centered = values - jnp.mean(values, axis=-1, keepdims=True)
    variance = jnp.mean(centered * centered, axis=-1, keepdims=True)
    return centered * lax.rsqrt(variance + 1e-05)


def contract_with(left, shard_piece):
    return jnp.dot(left, shard_piece, preferred_element_type=jnp.float32)


def contract_three(left, shard_piece):
    return jnp.einsum("fk,jkc->jfc", left, shard_piece, preferred_element_type=jnp.float32)


def body(
    token_ids,
    decoded_mask,
    levels_done,
    code_tables,
    mask_vectors,
    w_qkv,
    w_out,
    w_expand,
    w_depth,
    w_project,
    level_heads,
):
    frames = token_ids.shape[2]
    model_width = code_tables.shape[2]
    groups = lax.axis_size("level")
    level_index = lax.axis_index("level")
    local_rows = frames // groups
    head_dim = model_width // HEADS
    scale = head_dim ** (-0.5)
    id_row = token_ids[0, 0]
    flag_row = decoded_mask[0, 0]
    done_count = levels_done[0]
    own_table = code_tables[0]
    fill_row = mask_vectors[0].astype(jnp.float32)
    all_live = level_index < done_count
    current = level_index == done_count
    use_token = all_live | current & (flag_row == 1)
    codes = lax.broadcasted_iota(jnp.int32, (frames, own_table.shape[0]), 1)
    onehot = (id_row[:, None] == codes).astype(jnp.bfloat16)
    picked = jnp.dot(onehot, own_table, preferred_element_type=jnp.float32)
    level_terms = (
        jnp.where(use_token[:, None], picked, fill_row[None, :])
        .astype(jnp.bfloat16)
        .reshape(groups, local_rows, model_width)
    )
    received = lax.all_to_all(level_terms, "level", split_axis=0, concat_axis=0, tiled=True)
    own_rows = jnp.sum(received, axis=0, dtype=jnp.float32)
    normed = layer_norm(own_rows).astype(jnp.bfloat16)
    full_columns = gather_directly(w_qkv, "level", 2)
    projected = contract_three(
        normed, lax.all_gather(full_columns, "dp", axis=1, tiled=True)
    ).astype(jnp.bfloat16)
    queries = projected[0].reshape(local_rows, HEADS, head_dim)
    running_max = jnp.full((HEADS, local_rows), -1e30, jnp.float32)
    accumulated = jnp.zeros((local_rows, HEADS, head_dim), jnp.float32)
    key_piece, value_piece = side_by_side((projected[1], projected[2]), "level", 0, 1)
    piece_rows = key_piece.shape[0]
    key_three = key_piece.reshape(piece_rows, HEADS, head_dim)
    value_three = value_piece.reshape(piece_rows, HEADS, head_dim)
    scores = (
        jnp.einsum("qhd,khd->hqk", queries, key_three, preferred_element_type=jnp.float32) * scale
    )
    new_max = jnp.maximum(running_max, jnp.max(scores, axis=-1))
    shrink = jnp.exp(running_max - new_max)
    weights = jnp.exp(scores - new_max[:, :, None])
    weight_sum = jnp.sum(weights, axis=-1)
    added = jnp.einsum(
        "hqk,khd->qhd",
        weights.astype(jnp.bfloat16),
        value_three,
        preferred_element_type=jnp.float32,
    )
    accumulated = accumulated * shrink.T[:, :, None] + added
    running_max, weight_sum, accumulated = (new_max, weight_sum, accumulated)
    attended = (
        (accumulated / weight_sum.T[:, :, None])
        .reshape(local_rows, model_width)
        .astype(jnp.bfloat16)
    )
    out_full = gather_directly(w_out, "level", 0)
    after_attn = own_rows + jnp.dot(
        attended,
        lax.all_gather(out_full, "dp", axis=1, tiled=True),
        preferred_element_type=jnp.float32,
    )
    normed_two = layer_norm(after_attn).astype(jnp.bfloat16)
    gate_linear = contract_with(normed_two, lax.all_gather(w_expand, "dp", axis=0, tiled=True))
    gated = (gate_linear[:, :model_width] * jax.nn.sigmoid(gate_linear[:, model_width:])).astype(
        jnp.bfloat16
    )
    half_width = w_depth.shape[0] // 2
    padded = with_halo(gated, (("level", 0),), half_width)
    conv = jnp.zeros((local_rows, model_width), jnp.float32)
    for tap_index in range(w_depth.shape[0]):
        conv = conv + padded[tap_index : tap_index + local_rows].astype(jnp.float32) * w_depth[
            tap_index
        ].astype(jnp.float32)
    activated = (conv * jax.nn.sigmoid(conv)).astype(jnp.bfloat16)
    after_conv = after_attn + contract_with(
        activated, lax.all_gather(w_project, "dp", axis=0, tiled=True)
    )
    final_norm = layer_norm(after_conv).astype(jnp.bfloat16)
    own_head = level_heads[0]
    logits = jnp.dot(
        lax.all_gather(final_norm, "level", axis=0, tiled=True),
        own_head,
        preferred_element_type=jnp.float32,
    ).astype(jnp.bfloat16)
    return logits[None, None]


def solution(mesh):
    return jax.shard_map(
        body,
        mesh=mesh,
        in_specs=(
            P("dp", "level", None),
            P("dp", "level", None),
            P("dp"),
            P("level", None, None),
            P("level", None),
            P(None, "dp", "level"),
            P("level", "dp"),
            P("dp", None),
            P(),
            P("dp", None),
            P("level", None, None),
        ),
        out_specs=P("dp", "level", None, None),
        check_vma=False,
    )
```

profile of v0, /device:TPU:32, one launch (start us, length us, event | category | flops | bytes accessed | tf_op | source)
XLA Modules:
  0.0 499.3 jit_solution(8657905231968769645)
XLA Ops:
  6.5 0.9 broadcast_in_dim.57
  7.5 11.3 %all_to_all.15 = bf16[8,3,32,128]{3,2,1,0:T(8,128)(2,1)S(1)} all-to-all(bf16[8,3,32,128]{3,2,1,0:T(8,128)(2,1)S(1)} %broadcast_in_dim.57), channel_id=1, replica_groups=mesh['dp'=32,'level'=8] {'level'}, dimensions={0} | all-to-all | bytes 393216 | tf_op jit(solution)/shard_map/all_to_all | solution.py:11
  18.8 0.7 copy_bitcast_fusion
  19.6 0.7 broadcast_in_dim.61
  20.9 0.7 reduce.2
  21.6 0.7 or_reduce_fusion
  22.4 4.3 select_convert_fusion
  26.6 68.8 %all_to_all.16 = bf16[8,192,1024]{2,1,0:T(8,128)(2,1)S(1)} all-to-all(bf16[8,192,1024]{2,1,0:T(8,128)(2,1)S(1)} %bitcast.63), channel_id=1, replica_groups=mesh['dp'=32,'level'=8] {'level'}, dimensions={0} | all-to-all | bytes 6291456 | tf_op jit(solution)/shard_map/all_to_all | solution.py:97
  95.4 1.8 convert_reduce_fusion
  97.4 2.4 all-gather.7.cloned.1.call-done
  99.8 4.2 fusion.11
  104.2 0.9 pad_maximum_fusion
  105.2 11.6 %all_to_all.17 = bf16[8,128,32]{1,2,0:T(8,128)(2,1)S(1)} all-to-all(bf16[8,128,32]{1,2,0:T(8,128)(2,1)S(1)} %broadcast_in_dim.59), channel_id=1, replica_groups=mesh['dp'=32,'level'=8] {'level'}, dimensions={0} | all-to-all | bytes 131072 | tf_op jit(solution)/shard_map/all_to_all | solution.py:11
  116.8 0.6 copy_bitcast_fusion.1
  118.9 118.8 %all-gather.9.cloned.1.call-done = bf16[1536,2048]{1,0:T(8,128)(2,1)} async-done(((bf16[192,2048]{1,0:T(8,128)(2,1)}), bf16[1536,2048]{1,0:T(8,128)(2,1)}) %all-gather.9.cloned.1.call-update) | async-done | bytes 6291472 | tf_op jit(solution)/shard_map/all_gather | solution.py:31
  237.7 6.3 %fusion.45 = (bf16[1536,1024]{1,0:T(8,128)(2,1)}, bf16[1536,1024]{1,0:T(8,128)(2,1)}) fusion(bf16[1536,2048]{1,0:T(8,128)(2,1)} %all-gather.9.cloned.1.call-done), kind=kLoop, calls=%fused_computation.81 | loop fusion | bytes 12582912 | tf_op jit(solution)/shard_map/split | solution.py:31
  243.9 4.7 copy.27
  248.7 4.7 copy.26
  253.3 11.1 %multiply_reduce_fusion = (f32[16,192]{1,0:T(8,128)S(1)}, f32[16,192,1536]{2,1,0:T(8,128)}) fusion(bf16[192,16,64]{0,2,1:T(8,128)(2,1)S(1)} %bitcast.61, bf16[1536,16,64]{0,2,1:T(8,128)(2,1)} %bitcast.60), kind=kOutput, calls=%fused_computation.1 | convolution fusion | flops 613413888 | bytes 22425600 | tf_op jit(solution)/shard_map/qhd,khd->hqk/dot_general | solution.py:112
  264.4 9.6 %fusion = f32[16,192]{1,0:T(8,128)S(1)} fusion(f32[16,192,1536]{2,1,0:T(8,128)} %get-tuple-element.22, f32[16,192]{1,0:T(8,128)S(1)} %get-tuple-element.20), kind=kLoop, calls=%fused_computation.2 | loop fusion | flops 14152704 | bytes 18898944 | tf_op jit(solution)/shard_map/reduce_sum | solution.py:117
  274.0 11.1 %divide_convert_fusion = bf16[192,16,64]{0,2,1:T(8,128)(2,1)S(1)} fusion(bf16[1536,16,64]{0,2,1:T(8,128)(2,1)} %bitcast.62, f32[16,192,1536]{2,1,0:T(8,128)} %get-tuple-element.22, f32[16,192]{1,0:T(8,128)S(1)} %get-tuple-element.20, f32[192,16]{0,1:T(8,128)S(1)} %bitcast.65, f32[192,16]{0,1:T(8,128)S(1)} %get-tuple-element.19), kind=kOutput, calls=%fused_computation.23 | convolution fusion | flops 618725376 | bytes 22450176 | tf_op jit(solution)/shard_map/hqk,khd->qhd/dot_general | solution.py:118
  285.1 8.9 %all-gather.11.cloned.1.call-done = bf16[1024,1024]{0,1:T(8,128)(2,1)} async-done(((bf16[1024,32]{0,1:T(8,128)(2,1)}), bf16[1024,1024]{0,1:T(8,128)(2,1)}) %all-gather.11.cloned.1.call-update) | async-done | bytes 2097168 | tf_op jit(solution)/shard_map/all_gather | solution.py:134
  294.0 2.5 fusion.48
  296.8 58.2 %all-gather.13.cloned.1.call-done = bf16[1024,2048]{1,0:T(8,128)(2,1)} async-done(((bf16[32,2048]{1,0:T(8,128)(2,1)}), bf16[1024,2048]{1,0:T(8,128)(2,1)}) %all-gather.13.cloned.1.call-update) | async-done | bytes 4194320 | tf_op jit(solution)/shard_map/all_gather | solution.py:138
  355.0 3.2 fusion.29
  358.5 3.3 collective-permute-start.1
  361.8 3.7 collective-permute-start
  365.5 43.6 %all-gather.15.cloned.1.call-done = bf16[1024,1024]{1,0:T(8,128)(2,1)} async-done(((bf16[32,1024]{1,0:T(8,128)(2,1)}), bf16[1024,1024]{1,0:T(8,128)(2,1)}) %all-gather.15.cloned.1.call-update) | async-done | bytes 2097168 | tf_op jit(solution)/shard_map/all_gather | solution.py:151
  409.1 2.7 fusion.49
  412.0 0.9 multiply_convert_fusion
  413.0 71.7 %all-gather.17.cloned.1.call-done = bf16[1536,1024]{1,0:T(8,128)(2,1)} async-done(((bf16[192,1024]{1,0:T(8,128)(2,1)}), bf16[1536,1024]{1,0:T(8,128)(2,1)}) %all-gather.17.cloned.1.call-update) | async-done | bytes 3145744 | tf_op jit(solution)/shard_map/all_gather | solution.py:156
  484.6 7.8 %fusion.7 = bf16[1,1,1536,1024]{3,2,1,0:T(8,128)(2,1)} fusion(bf16[1536,1024]{1,0:T(8,128)(2,1)} %all-gather.17.cloned.1.call-done, bf16[1,1024,1024]{2,1,0:T(8,128)(2,1)} %param.21), kind=kOutput, calls=%fused_computation.13 | convolution fusion | flops 3222798336 | bytes 8388608 | tf_op jit(solution)/shard_map/dot_general | solution.py:155
  (38 shorter events, 2.6 us)
Async XLA Ops:
  6.5 15.8 %copy-start = (bf16[1,1024,1024]{2,1,0:T(8,128)(2,1)S(1)}, bf16[1,1024,1024]{2,1,0:T(8,128)(2,1)}, u32[]{:S(2)}) copy-start(bf16[1,1024,1024]{2,1,0:T(8,128)(2,1)} %param.14) | copy-start | bytes 6291460
  6.5 93.3 %all-gather.7.cloned.1.call-start = ((), (), s32[]{:S(2)}) async-start(), calls=%async_computation.3 | async-start | bytes 6488064 | tf_op jit(solution)/shard_map/all_gather | solution.py:102
  19.5 218.2 %all-gather.9.cloned.1.call-start = ((), (), s32[]{:S(2)}) async-start(), calls=%async_computation.4 | async-start | bytes 7077888 | tf_op jit(solution)/shard_map/all_gather | solution.py:31
  104.1 1.1 copy-start.3
  105.1 188.9 %all-gather.11.cloned.1.call-start = ((), (), s32[]{:S(2)}) async-start(), calls=%async_computation.5 | async-start | bytes 2162688 | tf_op jit(solution)/shard_map/all_gather | solution.py:134
  117.5 237.5 %all-gather.13.cloned.1.call-start = ((), (), s32[]{:S(2)}) async-start(), calls=%async_computation.6 | async-start | bytes 4325376 | tf_op jit(solution)/shard_map/all_gather | solution.py:138
  118.1 291.0 %all-gather.15.cloned.1.call-start = ((), (), s32[]{:S(2)}) async-start(), calls=%async_computation.7 | async-start | bytes 2162688 | tf_op jit(solution)/shard_map/all_gather | solution.py:151
  118.7 366.0 %all-gather.17.cloned.1.call-start = ((), (), s32[]{:S(2)}) async-start(), calls=%async_computation.8 | async-start | bytes 3538944 | tf_op jit(solution)/shard_map/all_gather | solution.py:156
  296.8 68.7 %copy-start.2 = (bf16[5,1024]{1,0:T(8,128)(2,1)S(1)}, bf16[5,1024]{1,0:T(8,128)(2,1)}, u32[]{:S(2)}) copy-start(bf16[5,1024]{1,0:T(8,128)(2,1)} %param.19) | copy-start | bytes 30724
  358.5 50.6 %collective-permute-start.1 = (bf16[2,1024]{1,0:T(2,128)(2,1)S(1)}, bf16[2,1024]{1,0:T(2,128)(2,1)S(1)}, u32[]{:S(2)}, u32[]{:S(2)}) collective-permute-start(bf16[2,1024]{1,0:T(2,128)(2,1)S(1)} %get-tuple-element.13), channel_id=1, source_target_pairs={{1,0},{2,1},{3,2},{4,3},{5,4},{6,5},{7,6},{9,8},{10,9},{11,10},{12... | collective-permute-start | bytes 12296 | tf_op jit(solution)/shard_map/ppermute | solution.py:42
  361.8 47.3 %collective-permute-start = (bf16[2,1024]{1,0:T(2,128)(2,1)S(1)}, bf16[2,1024]{1,0:T(2,128)(2,1)S(1)}, u32[]{:S(2)}, u32[]{:S(2)}) collective-permute-start(bf16[2,1024]{1,0:T(2,128)(2,1)S(1)} %get-tuple-element.12), channel_id=1, source_target_pairs={{0,1},{1,2},{2,3},{3,4},{4,5},{5,6},{6,7},{8,9},{9,10},{10,11},{11... | collective-permute-start | bytes 12296 | tf_op jit(solution)/shard_map/ppermute | solution.py:41
  484.6 7.8 %copy-start.1 = (bf16[1,1024,1024]{2,1,0:T(8,128)(2,1)S(1)}, bf16[1,1024,1024]{2,1,0:T(8,128)(2,1)}, u32[]{:S(2)}) copy-start(bf16[1,1024,1024]{2,1,0:T(8,128)(2,1)} %param.14) | copy-start | bytes 6291460
Sparse Core Ops, SparseCore 0:
  19.6 80.1 all-gather.6
  105.2 132.3 all-gather.8
  240.2 53.7 all-gather.10
  296.4 58.5 all-gather.12
  357.4 51.6 all-gather.14
  413.1 71.4 all-gather.16
where the time goes:
time: 502 us; the launch traced here: 499 us
  waiting for transfers between devices  305 us (61%)
  blocking collectives  91.7 us (18%)
  matrix products  46.9 us (9%)
  local copies, waits for them, and re-layouts  18.2 us (4%)
  other arithmetic  16.4 us (3%)
  between operations  14.3 us (3%)
  starting transfers between devices  7.17 us (1%)
    all_gather x1, waiting for transfers between devices, side_by_side(): lax.all_gather(both, axis, axis=dim, tiled=True)  119 us
    all_gather x1, waiting for transfers between devices, body(): lax.all_gather(final_norm, 'level', axis=0, tiled=True)  71.7 us
    all_to_all x1, blocking collectives, body(): lax.all_to_all(level_terms, 'level', split_axis=0, concat_axis=0, tiled=T...  68.8 us
    all_gather x1, waiting for transfers between devices, body(): lax.all_gather(w_expand, 'dp', axis=0, tiled=True)  58.2 us
    all_gather x1, waiting for transfers between devices, body(): lax.all_gather(w_project, 'dp', axis=0, tiled=True)  43.6 us
    all_to_all x2, blocking collectives, copy_for_each(): return lax.all_to_all(copies, axis, split_axis=0, concat_axis=0, tiled=True)  23 us
    split x3, local copies, waits for them, and re-layouts, side_by_side(): jnp.split(lax.all_gather(both, axis, axis=dim, tiled=True), ends, axis=al...  15.7 us
    dot_general x1, matrix products, body(): jnp.einsum('hqk,khd->qhd', weights.astype(jnp.bfloat16), value_three, pre...  11.1 us
  transfers between devices with their start and end apart: 8, of which 6 were waited for; matrix products, arithmetic and copies ran while one was open for 13% of the time, Pallas kernels for 0%

commit v1 on v0

v1 whole, which is shorter than its diff:
```python
import jax
import jax.numpy as jnp
from jax import lax
from jax.experimental import pallas as pl
from jax.experimental.pallas import tpu as pltpu
from jax.sharding import PartitionSpec as P

MESH = pl.DeviceIdType.MESH
BF16, F32 = jnp.bfloat16, jnp.float32

HEADS = 16
NZ, NY, NC = 4, 4, 2
NX, NL = 4, 2
LANES = 128
COPIES = 128


def layer_norm(values):
    centered = values - jnp.mean(values, axis=-1, keepdims=True)
    variance = jnp.mean(centered * centered, axis=-1, keepdims=True)
    return centered * lax.rsqrt(variance + 1e-05)


def step_kernel(
    sel_ref,
    fill_ref,
    taps_ref,
    table_hbm,
    wqkv_hbm,
    wout_hbm,
    wexp_hbm,
    wproj_hbm,
    head_hbm,
    out_hbm,
    table,
    head,
    weights,
    terms,
    partial,
    zsend,
    zrecv,
    own,
    normed,
    qkv_s,
    qkv_r,
    att_s,
    att_r,
    after,
    gated,
    halo,
    padded,
    active,
    final,
    staged,
    load_sem,
    store_sem,
    send_sem,
    recv_sem,
):
    groups = NX * NL
    rows, width = own.shape
    frames = rows * groups
    half = width // 2
    shard = weights.shape[3]

    dp = lax.axis_index("dp")
    lv = lax.axis_index("level")
    core = lax.rem(dp, NC)
    yy = lax.rem(dp // NC, NY)
    zh = dp // (NC * NY)
    xx, zl = lv // NL, lax.rem(lv, NL)
    zy = zh * NY + yy

    def level_of(dx, dz):
        return lax.rem(xx + dx + NX, NX) * NL + lax.rem(zl + dz, NL)

    def dp_of(dz, dy, dc):
        return (lax.rem(zh + dz + NZ, NZ) * NY + lax.rem(yy + dy + NY, NY)) * NC + lax.rem(core + dc, NC)

    x_up, x_down, z_mate = {"level": level_of(1, 0)}, {"level": level_of(-1, 0)}, {"level": level_of(0, 1)}
    z_up, z_down = {"dp": dp_of(1, 0, 0)}, {"dp": dp_of(-1, 0, 0)}
    y_up, y_down = {"dp": dp_of(0, 1, 0)}, {"dp": dp_of(0, -1, 0)}
    core_mate = {"dp": dp_of(0, 0, 1)}

    lane_at = pl.ds(pl.multiple_of(lv * LANES, LANES), LANES)
    loads = [
        pltpu.make_async_copy(table_hbm, table, load_sem.at[0]),
        pltpu.make_async_copy(wqkv_hbm, weights.at[zy, core, pl.ds(0, 3), :, lane_at], load_sem.at[1]),
        pltpu.make_async_copy(wout_hbm, weights.at[zy, core, 3, :, lane_at], load_sem.at[2]),
        pltpu.make_async_copy(wexp_hbm.at[:, pl.ds(0, width)], weights.at[zy, core, 4], load_sem.at[3]),
        pltpu.make_async_copy(wexp_hbm.at[:, pl.ds(width, width)], weights.at[zy, core, 5], load_sem.at[4]),
        pltpu.make_async_copy(wproj_hbm, weights.at[zy, core, 6], load_sem.at[5]),
        pltpu.make_async_copy(head_hbm, head, load_sem.at[6]),
    ]
    for load in loads:
        load.start()

    barrier = pltpu.get_barrier_semaphore()
    for k in range(1, groups):
        pl.semaphore_signal(barrier, inc=1, device_id={"level": level_of(k // NL, k % NL)}, device_id_type=MESH)
    for peer in (z_up, z_down, y_up, y_down, core_mate):
        pl.semaphore_signal(barrier, inc=1, device_id=peer, device_id_type=MESH)
    pl.semaphore_wait(barrier, groups + 4)

    used = [0]
    sent = []

    def make(src, dst, device, index):
        return pltpu.make_async_remote_copy(
            src_ref=src,
            dst_ref=dst,
            send_sem=send_sem.at[index],
            recv_sem=recv_sem.at[index],
            device_id=device,
            device_id_type=MESH,
        )

    def send(src, dst, device):
        copy = make(src, dst, device, used[0])
        used[0] += 1
        copy.start()
        sent.append(copy)
        return copy

    for load in loads[1:3]:
        load.wait()
    first = weights.at[zy, core, pl.ds(0, 4), :, lane_at]
    columns = [send(first, first, {"level": level_of(k // NL, k % NL)}) for k in range(1, groups)]

    codes = lax.broadcasted_iota(jnp.int32, (rows, table.shape[0]), 1).astype(F32)
    slots = lax.broadcasted_iota(jnp.int32, (rows, groups), 1)

    def term(dx, dz):
        dest = level_of(dx, dz)
        ids = jnp.sum(jnp.where(slots == dest, sel_ref[...], 0.0), axis=1, keepdims=True)
        onehot = jnp.where(ids == codes, 1.0, 0.0).astype(BF16)
        picked = jnp.dot(onehot, table[...], preferred_element_type=F32)
        terms[dest] = jnp.where(ids < 0.0, fill_ref[...].astype(F32), picked).astype(BF16)

    def col(d):
        return pl.ds(d * half, half)

    def ring_send(step, d, q):
        dx = -step if d == 0 else step
        block = terms.at[level_of(dx + NX, 1 - q), :, col(d)]
        return send(block, partial.at[d, step - 1, q], x_up if d == 0 else x_down)

    loads[0].wait()
    ring = {}
    for q in range(2):

        @pl.loop(0, 2)
        def _(i):
            term(2 * i + NX - 1, 1 - q)

        for d in range(2):
            ring[1, d, q] = ring_send(1, d, q)

    @pl.loop(0, 4)
    def _(i):
        term(2 + 2 * (i // 2), lax.rem(i + 1, 2))

    spans = (pl.ds(0, 3), pl.ds(3, 4))
    low, high = pl.ds(0, shard // 2), pl.ds(shard // 2, shard // 2)

    def place(dz, dy, g, part=None):
        at = lax.rem(zh + dz + NZ, NZ) * NY + lax.rem(yy + dy + NY, NY)
        if part is None:
            return weights.at[at, core, spans[g]]
        return weights.at[at, core, spans[g], part]

    zcopy, zfar, ycopy, yfar, mate = {}, {}, {}, {}, {}

    def z_start(g):
        block = place(0, 0, g)
        zcopy[g] = (send(block, block, z_up), send(block, block, z_down))

    def z_forward(g):
        for copy in zcopy[g]:
            copy.wait_recv()
        one, two = place(-1, 0, g, low), place(1, 0, g, high)
        zfar[g] = (send(one, one, z_up), send(two, two, z_down))

    def z_last(g):
        for copy in zfar[g]:
            copy.wait_recv()

    def y_start(g, dz):
        block = place(dz, 0, g)
        ycopy[g, dz] = (send(block, block, y_up), send(block, block, y_down))

    def y_forward(g, dz):
        for copy in ycopy[g, dz]:
            copy.wait_recv()
        one, two = place(dz, -1, g, low), place(dz, 1, g, high)
        yfar[g, dz] = (send(one, one, y_up), send(two, two, y_down))

    def mate_start(g, dz):
        for copy in yfar[g, dz]:
            copy.wait_recv()
        plane = weights.at[pl.ds(lax.rem(zh + dz + NZ, NZ) * NY, NY), core, spans[g]]
        mate[g, dz] = send(plane, plane, core_mate)

    def mate_wait(g):
        for dz in (0, -1, 1, 2):
            mate[g, dz].wait_recv()

    for load in loads[3:6]:
        load.wait()
    for copy in columns:
        copy.wait_recv()
    z_start(0)
    y_start(0, 0)
    z_start(1)
    y_start(1, 0)

    def ring_next(step, q):
        for d in range(2):
            ring[step, d, q].wait_recv()
            dest = level_of(-step - 1 + 2 * NX if d == 0 else step + 1, 1 - q)
            total = terms[dest, :, col(d)].astype(F32) + partial[d, step - 1, q].astype(F32)
            if step < NX - 1:
                terms[dest, :, col(d)] = total.astype(BF16)
                ring[step + 1, d, q] = ring_send(step + 1, d, q)
            elif q == 0:
                zsend[d] = total.astype(BF16)
                ring["z", d] = send(zsend.at[d], zrecv.at[d], z_mate)
            else:
                own[:, col(d)] = total

    ring_next(1, 0)
    y_forward(0, 0)
    ring_next(1, 1)
    z_forward(0)
    y_start(0, -1)
    y_start(0, 1)
    ring_next(2, 0)
    y_forward(1, 0)
    mate_start(0, 0)
    ring_next(2, 1)
    z_last(0)
    y_start(0, 2)
    ring_next(3, 0)
    y_forward(0, -1)
    y_forward(0, 1)
    z_forward(1)
    y_start(1, -1)
    y_start(1, 1)
    ring_next(3, 1)
    for d in range(2):
        ring["z", d].wait_recv()
        own[:, col(d)] += zrecv[d].astype(F32)

    chunk = 32

    @pl.loop(0, rows // chunk)
    def _(i):
        at = pl.ds(pl.multiple_of(i * chunk, chunk), chunk)
        normed[at] = layer_norm(own[at]).astype(BF16)

    mate_start(0, -1)
    mate_start(0, 1)
    y_forward(0, 2)
    z_last(1)
    y_start(1, 2)
    mate_start(0, 2)
    mate_wait(0)

    def weight(j, start, size):
        return weights[:, :, j, :, pl.ds(start, size)].reshape(width, size)

    def project(j):
        size = half
        for h in range(width // size):
            product = jnp.dot(normed[...], weight(j, h * size, size), preferred_element_type=F32)
            for i in range(size // LANES):
                qkv_s[h * (size // LANES) + i, j] = product[:, i * LANES : (i + 1) * LANES].astype(BF16)

    project(1)
    project(2)
    order = (4, 5, 2, 3, 6, 7, 1)
    kv_copies, q_base = [], None
    for k in order:
        dest = level_of(k // NL, k % NL)
        kv_copies.append(send(qkv_s.at[dest, pl.ds(1, 2)], qkv_r.at[lv, pl.ds(1, 2)], {"level": dest}))
    project(0)
    q_base = used[0]
    for k in range(1, groups):
        dest = level_of(k // NL, k % NL)
        send(qkv_s.at[dest, 0], qkv_r.at[lv, 0], {"level": dest})
    qkv_r[lv] = qkv_s[lv]
    y_forward(1, -1)
    y_forward(1, 1)
    mate_start(1, 0)
    for copy in kv_copies:
        copy.wait_recv()

    head_dim = width // HEADS
    att_base = used[0]
    used[0] += groups - 1

    def attend(src):
        lane = lax.broadcasted_iota(jnp.int32, (rows, LANES), 1)
        query = qkv_r[src, 0].astype(F32) * head_dim ** (-0.5)
        keys = qkv_r[:, 1].reshape(frames, LANES)
        values = qkv_r[:, 2].reshape(frames, LANES)
        mixed = []
        for h in range(LANES // head_dim):
            mine = (lane // head_dim) == h
            masked = jnp.where(mine, query, 0.0).astype(BF16)
            scores = lax.dot_general(masked, keys, (((1,), (1,)), ((), ())), preferred_element_type=F32)
            grown = jnp.exp(scores - jnp.max(scores, axis=-1, keepdims=True))
            total = jnp.sum(grown, axis=-1, keepdims=True)
            mixture = jnp.dot(grown.astype(BF16), values, preferred_element_type=F32) / total
            mixed.append((mine, mixture))
        merged = mixed[0][1]
        for mine, mixture in mixed[1:]:
            merged = jnp.where(mine, mixture, merged)
        return merged.astype(BF16)

    def att_copy(k):
        src = level_of(NX - k // NL, NL - lax.rem(k, NL))
        return src, make(att_s.at[src], att_r.at[:, lane_at], {"level": src}, att_base + k - 1)

    def attend_peers(first_k, last_k):
        @pl.loop(first_k, last_k)
        def _(k):
            src, copy = att_copy(k)
            make(qkv_s.at[src, 0], qkv_r.at[src, 0], {"level": src}, q_base + k - 1).wait_recv()
            att_s[src] = attend(src)
            copy.start()

    attend_peers(1, 4)
    y_forward(1, 2)
    mate_start(1, -1)
    mate_start(1, 1)
    attend_peers(4, groups)
    att_r[:, lane_at] = attend(lv)
    mate_start(1, 2)
    mate_wait(1)

    @pl.loop(1, groups)
    def _(k):
        _, copy = att_copy(k)
        copy.wait_recv()

    attended = lax.dot_general(
        att_r[...], weight(3, 0, width), (((1,), (1,)), ((), ())), preferred_element_type=F32
    )
    after[...] = own[...] + attended

    @pl.loop(0, rows // chunk)
    def _(i):
        at = pl.ds(pl.multiple_of(i * chunk, chunk), chunk)
        normed[at] = layer_norm(after[at]).astype(BF16)

    edge = padded.shape[0] - rows
    edge = edge // 2
    piece = 256
    for h in range(width // piece):
        linear = jnp.dot(normed[...], weight(4, h * piece, piece), preferred_element_type=F32)
        gate = jnp.dot(normed[...], weight(5, h * piece, piece), preferred_element_type=F32)
        value = (linear * jax.nn.sigmoid(gate)).astype(BF16)
        gated[:, pl.ds(h * piece, piece)] = value
        padded[pl.ds(edge, rows), pl.ds(h * piece, piece)] = value.astype(F32)
    tile = halo.shape[1]
    after_me, before_me = lax.rem(lv + 1, groups), lax.rem(lv + groups - 1, groups)
    edges = (
        send(gated.at[pl.ds(rows - tile, tile)], halo.at[0], {"level": after_me}),
        send(gated.at[pl.ds(0, tile)], halo.at[1], {"level": before_me}),
    )

    taps = taps_ref.shape[0]
    reach = taps // 2

    def convolve(start, count):
        conv = jnp.zeros((count, width), F32)
        for t in range(taps):
            conv = conv + padded[pl.ds(edge + start + t - reach, count)] * taps_ref[pl.ds(t, 1)].astype(F32)
        active[pl.ds(start, count)] = (conv * jax.nn.sigmoid(conv)).astype(BF16)

    for start in range(tile, rows - tile, 32):
        convolve(start, 32)
    for copy in edges:
        copy.wait_recv()
    padded[pl.ds(0, edge)] = jnp.where(lv > 0, halo[0, pl.ds(tile - edge, edge)].astype(F32), 0.0)
    padded[pl.ds(edge + rows, edge)] = jnp.where(lv < groups - 1, halo[1, pl.ds(0, edge)].astype(F32), 0.0)
    convolve(0, tile)
    convolve(rows - tile, tile)
    after[...] += jnp.dot(active[...], weight(6, 0, width), preferred_element_type=F32)

    @pl.loop(0, rows // chunk)
    def _(i):
        at = pl.ds(pl.multiple_of(i * chunk, chunk), chunk)
        final[lv, at] = layer_norm(after[at]).astype(BF16)

    stores = []

    def logits(block):
        for h in range(2):
            product = jnp.dot(final[block], head[:, col(h)], preferred_element_type=F32)
            staged[block, :, col(h)] = product.astype(BF16)
        at = pl.ds(pl.multiple_of(block * rows, rows), rows)
        copy = pltpu.make_async_copy(staged.at[block], out_hbm.at[at], store_sem.at[len(stores)])
        copy.start()
        stores.append(copy)

    mine = final.at[lv]
    from_down, from_up, from_mate = send(mine, mine, x_up), send(mine, mine, x_down), send(mine, mine, z_mate)
    top, bottom = pl.ds(0, rows // 2), pl.ds(rows // 2, rows // 2)
    loads[6].wait()
    logits(lv)
    from_down.wait_recv()
    from_up.wait_recv()
    one, two = final.at[level_of(-1, 0), top], final.at[level_of(1, 0), bottom]
    far = (send(one, one, x_up), send(two, two, x_down))
    from_mate.wait_recv()
    mate_block = final.at[level_of(0, 1)]
    mate_down, mate_up = send(mate_block, mate_block, x_up), send(mate_block, mate_block, x_down)
    logits(level_of(-1, 0))
    logits(level_of(1, 0))
    for copy in far:
        copy.wait_recv()
    opposite = final.at[level_of(2, 0)]
    last = send(opposite, opposite, z_mate)
    logits(level_of(0, 1))
    logits(level_of(2, 0))
    mate_down.wait_recv()
    logits(level_of(-1, 1))
    mate_up.wait_recv()
    logits(level_of(1, 1))
    last.wait_recv()
    logits(level_of(2, 1))

    for copy in sent:
        copy.wait_send()

    @pl.loop(1, groups)
    def _(k):
        _, copy = att_copy(k)
        copy.wait_send()

    for copy in stores:
        copy.wait()


def body(
    token_ids,
    decoded_mask,
    levels_done,
    code_tables,
    mask_vectors,
    w_qkv,
    w_out,
    w_expand,
    w_depth,
    w_project,
    level_heads,
):
    frames = token_ids.shape[2]
    width = code_tables.shape[2]
    groups = lax.axis_size("level")
    level = lax.axis_index("level")
    rows = frames // groups
    done = levels_done[0]
    use_token = (level < done) | (level == done) & (decoded_mask[0, 0] == 1)
    sel = jnp.where(use_token, token_ids[0, 0], -1).astype(F32).reshape(groups, rows).T
    shard = w_project.shape[0]
    tile, edge = 16, 8
    vmem = pl.BlockSpec(memory_space=pltpu.VMEM)
    hbm = pl.BlockSpec(memory_space=pl.ANY)
    logits = pl.pallas_call(
        step_kernel,
        out_shape=jax.ShapeDtypeStruct((frames, level_heads.shape[2]), BF16),
        in_specs=[vmem] * 3 + [hbm] * 6,
        out_specs=hbm,
        scratch_shapes=[
            pltpu.VMEM(code_tables.shape[1:], BF16),
            pltpu.VMEM(level_heads.shape[1:], BF16),
            pltpu.VMEM((NZ * NY, NC, 7, shard, width), BF16),
            pltpu.VMEM((groups, rows, width), BF16),
            pltpu.VMEM((2, NX - 1, 2, rows, width // 2), BF16),
            pltpu.VMEM((2, rows, width // 2), BF16),
            pltpu.VMEM((2, rows, width // 2), BF16),
            pltpu.VMEM((rows, width), F32),
            pltpu.VMEM((rows, width), BF16),
            pltpu.VMEM((groups, 3, rows, LANES), BF16),
            pltpu.VMEM((groups, 3, rows, LANES), BF16),
            pltpu.VMEM((groups, rows, LANES), BF16),
            pltpu.VMEM((rows, width), BF16),
            pltpu.VMEM((rows, width), F32),
            pltpu.VMEM((rows, width), BF16),
            pltpu.VMEM((2, tile, width), BF16),
            pltpu.VMEM((rows + 2 * edge, width), F32),
            pltpu.VMEM((rows, width), BF16),
            pltpu.VMEM((groups, rows, width), BF16),
            pltpu.VMEM((groups, rows, width), BF16),
            pltpu.SemaphoreType.DMA((7,)),
            pltpu.SemaphoreType.DMA((groups,)),
            pltpu.SemaphoreType.DMA((COPIES,)),
            pltpu.SemaphoreType.DMA((COPIES,)),
        ],
        compiler_params=pltpu.CompilerParams(
            collective_id=0, has_side_effects=True, vmem_limit_bytes=60 * 1024 * 1024
        ),
    )(
        sel,
        mask_vectors,
        w_depth,
        code_tables[0],
        w_qkv,
        w_out.T,
        w_expand,
        w_project,
        level_heads[0],
    )
    return logits[None, None]


def solution(mesh):
    return jax.shard_map(
        body,
        mesh=mesh,
        in_specs=(
            P("dp", "level", None),
            P("dp", "level", None),
            P("dp"),
            P("level", None, None),
            P("level", None),
            P(None, "dp", "level"),
            P("level", "dp"),
            P("dp", None),
            P(),
            P("dp", None),
            P("level", None, None),
        ),
        out_specs=P("dp", "level", None, None),
        check_vma=False,
    )
```

time: 502 us -> 136 us (0.27)
  waiting for transfers between devices: 305 us -> 0 us
  Pallas kernels: 0 us -> 129 us
  blocking collectives: 91.7 us -> 0 us
  matrix products: 46.9 us -> 0 us
  other arithmetic: 16.4 us -> 0.74 us
  between operations: 14.3 us -> 0.67 us
  local copies, waits for them, and re-layouts: 18.2 us -> 4.69 us
  starting transfers between devices: 7.17 us -> 0 us
    all_gather x6 -> x0, waiting for transfers between devices: 303 us -> none  [the longest x1 119 us: side_by_side(): lax.all_gather(both, axis, axis=dim, tiled=True)]
    pallas_call x0 -> x1, Pallas kernels: none -> 129 us  [body(): pl.pallas_call(step_kernel, out_shape=jax.ShapeDtypeStruct((frames, level...]
    all_to_all x3 -> x0, blocking collectives: 91.7 us -> none  [the longest x1 68.8 us: body(): lax.all_to_all(level_terms, 'level', split_axis=0, concat_axis=0, tiled=T...]
    dot_general x8 -> x0, matrix products: 46.9 us -> none  [the longest x1 11.1 us: body(): jnp.einsum('hqk,khd->qhd', weights.astype(jnp.bfloat16), value_three, pre...]
    split x3 -> x0, local copies, waits for them, and re-layouts: 15.7 us -> none  [side_by_side(): jnp.split(lax.all_gather(both, axis, axis=dim, tiled=True), ends, axis=al...]
    reduce_sum x5 -> x0, other arithmetic: 12.1 us -> none  [the longest x1 9.62 us: body(): weight_sum = jnp.sum(weights, axis=-1)]
    ppermute x2 -> x0, starting transfers between devices: 6.96 us -> none  [the longest x1 3.7 us: with_halo(): before = lax.ppermute(last, axis, up)]
  transfers between devices with their start and end apart: 8 -> 0, of which waited for: 6 -> 0; matrix products, arithmetic and copies ran while one was open for 13% -> 0% of each run, Pallas kernels for 0% -> 0%
where the time goes in v1:
time: 136 us; the launch traced here: 135 us
  Pallas kernels  129 us (95%)
  local copies, waits for them, and re-layouts  4.69 us (3%)
    pallas_call x1, Pallas kernels, body(): pl.pallas_call(step_kernel, out_shape=jax.ShapeDtypeStruct((frames, level...  129 us
    unnamed x1, local copies, waits for them, and re-layouts  3.86 us

profile of v1, /device:TPU:32, one launch (start us, length us, event | category | flops | bytes accessed | tf_op | source)
XLA Modules:
  0.0 135.0 jit_solution(3299842651637042619)
XLA Ops:
  0.7 0.7 convert_reduce_fusion
  1.4 0.1 reshape.11
  1.5 0.8 copy.12
  2.2 128.9 %shard_map.109 = bf16[1536,1024]{1,0:T(8,128)(2,1)} custom-call(f32[192,8]{1,0:T(8,128)} %bitcast.11, bf16[1,1024]{1,0:T(2,128)(2,1)} %fill_ref.1, bf16[5,1024]{1,0:T(8,128)(2,1)} %taps_ref.1, bf16[1024,1024]{1,0:T(8,128)(2,1)} %bitcast.9, bf16[3,32,128]{2,1,0:T(8,128)(2,1)} %wqkv_hbm.1, bf16[32,128]{1,0:T(8,128)(2,1)} %bitcast.12, ...), custom_call_target="tpu_custom_call" | custom-call | tf_op jit(solution)/shard_map/pallas_call | solution.py:472
  131.2 3.9 %copy.15 = bf16[1,1,1536,1024]{3,2,1,0:T(8,128)(2,1)} copy(bf16[1,1,1536,1024]{3,2,1,0:T(8,128)(2,1)} %bitcast.8) | data formatting | bytes 6291456

commit v2 on v1

--- a/solution.py
+++ b/solution.py
@@ -12,7 +12,7 @@
 NZ, NY, NC = 4, 4, 2
 NX, NL = 4, 2
 LANES = 128
-COPIES = 128
+COPIES = 192
 
 
 def layer_norm(values):
@@ -100,8 +100,6 @@
         pl.semaphore_signal(barrier, inc=1, device_id={"level": level_of(k // NL, k % NL)}, device_id_type=MESH)
     for peer in (z_up, z_down, y_up, y_down, core_mate):
         pl.semaphore_signal(barrier, inc=1, device_id=peer, device_id_type=MESH)
-    pl.semaphore_wait(barrier, groups + 4)
-
     used = [0]
     sent = []
 
@@ -122,11 +120,6 @@
         sent.append(copy)
         return copy
 
-    for load in loads[1:3]:
-        load.wait()
-    first = weights.at[zy, core, pl.ds(0, 4), :, lane_at]
-    columns = [send(first, first, {"level": level_of(k // NL, k % NL)}) for k in range(1, groups)]
-
     codes = lax.broadcasted_iota(jnp.int32, (rows, table.shape[0]), 1).astype(F32)
     slots = lax.broadcasted_iota(jnp.int32, (rows, groups), 1)
 
@@ -145,22 +138,14 @@
         block = terms.at[level_of(dx + NX, 1 - q), :, col(d)]
         return send(block, partial.at[d, step - 1, q], x_up if d == 0 else x_down)
 
+    ring = {}
     loads[0].wait()
-    ring = {}
-    for q in range(2):
-
-        @pl.loop(0, 2)
-        def _(i):
-            term(2 * i + NX - 1, 1 - q)
-
-        for d in range(2):
-            ring[1, d, q] = ring_send(1, d, q)
 
     @pl.loop(0, 4)
     def _(i):
-        term(2 + 2 * (i // 2), lax.rem(i + 1, 2))
-
-    spans = (pl.ds(0, 3), pl.ds(3, 4))
+        term(2 * lax.rem(i, 2) + NX - 1, 1 - i // 2)
+
+    spans = (pl.ds(1, 2), pl.ds(0, 1), pl.ds(3, 1), pl.ds(4, 3))
     low, high = pl.ds(0, shard // 2), pl.ds(shard // 2, shard // 2)
 
     def place(dz, dy, g, part=None):
@@ -204,15 +189,6 @@
     def mate_wait(g):
         for dz in (0, -1, 1, 2):
             mate[g, dz].wait_recv()
-
-    for load in loads[3:6]:
-        load.wait()
-    for copy in columns:
-        copy.wait_recv()
-    z_start(0)
-    y_start(0, 0)
-    z_start(1)
-    y_start(1, 0)
 
     def ring_next(step, q):
         for d in range(2):
@@ -228,25 +204,61 @@
             else:
                 own[:, col(d)] = total
 
+    pl.semaphore_wait(barrier, groups + 4)
+    for load in loads[1:6]:
+        load.wait()
+    first = weights.at[zy, core, pl.ds(0, 4), :, lane_at]
+    columns = [send(first, first, {"level": level_of(k // NL, k % NL)}) for k in range(1, groups)]
+    for q in range(2):
+        for d in range(2):
+            ring[1, d, q] = ring_send(1, d, q)
+    y_start(3, 0)
+
+    @pl.loop(0, 4)
+    def _(i):
+        term(2 + 2 * (i // 2), lax.rem(i + 1, 2))
+
+    for copy in columns:
+        copy.wait_recv()
+    z_start(0)
+    y_start(0, 0)
+    z_start(1)
+    y_start(1, 0)
     ring_next(1, 0)
+    y_forward(3, 0)
     y_forward(0, 0)
     ring_next(1, 1)
     z_forward(0)
     y_start(0, -1)
     y_start(0, 1)
-    ring_next(2, 0)
     y_forward(1, 0)
-    mate_start(0, 0)
-    ring_next(2, 1)
-    z_last(0)
-    y_start(0, 2)
-    ring_next(3, 0)
-    y_forward(0, -1)
-    y_forward(0, 1)
     z_forward(1)
     y_start(1, -1)
     y_start(1, 1)
+    z_start(2)
+    y_start(2, 0)
+    z_start(3)
+    ring_next(2, 0)
+    mate_start(0, 0)
+    z_last(0)
+    y_start(0, 2)
+    z_last(1)
+    y_start(1, 2)
+    ring_next(2, 1)
+    y_forward(0, -1)
+    y_forward(0, 1)
+    mate_start(1, 0)
+    ring_next(3, 0)
+    y_forward(1, -1)
+    y_forward(1, 1)
+    y_forward(0, 2)
     ring_next(3, 1)
+    y_forward(1, 2)
+    mate_start(0, -1)
+    mate_start(0, 1)
+    z_forward(2)
+    y_start(2, -1)
+    y_start(2, 1)
     for d in range(2):
         ring["z", d].wait_recv()
         own[:, col(d)] += zrecv[d].astype(F32)
@@ -258,12 +270,13 @@
         at = pl.ds(pl.multiple_of(i * chunk, chunk), chunk)
         normed[at] = layer_norm(own[at]).astype(BF16)
 
-    mate_start(0, -1)
-    mate_start(0, 1)
-    y_forward(0, 2)
-    z_last(1)
-    y_start(1, 2)
+    mate_start(1, -1)
+    mate_start(1, 1)
+    z_forward(3)
+    y_start(3, -1)
+    y_start(3, 1)
     mate_start(0, 2)
+    mate_start(1, 2)
     mate_wait(0)
 
     def weight(j, start, size):
@@ -283,15 +296,22 @@
     for k in order:
         dest = level_of(k // NL, k % NL)
         kv_copies.append(send(qkv_s.at[dest, pl.ds(1, 2)], qkv_r.at[lv, pl.ds(1, 2)], {"level": dest}))
+    mate_wait(1)
     project(0)
     q_base = used[0]
     for k in range(1, groups):
         dest = level_of(k // NL, k % NL)
         send(qkv_s.at[dest, 0], qkv_r.at[lv, 0], {"level": dest})
     qkv_r[lv] = qkv_s[lv]
-    y_forward(1, -1)
-    y_forward(1, 1)
-    mate_start(1, 0)
+    z_last(2)
+    y_start(2, 2)
+    y_forward(2, 0)
+    mate_start(3, 0)
+    y_forward(2, -1)
+    y_forward(2, 1)
+    mate_start(2, 0)
+    z_last(3)
+    y_start(3, 2)
     for copy in kv_copies:
         copy.wait_recv()
 
@@ -330,14 +350,21 @@
             att_s[src] = attend(src)
             copy.start()
 
-    attend_peers(1, 4)
-    y_forward(1, 2)
-    mate_start(1, -1)
-    mate_start(1, 1)
-    attend_peers(4, groups)
+    attend_peers(1, 3)
+    y_forward(2, 2)
+    y_forward(3, -1)
+    y_forward(3, 1)
+    mate_start(2, -1)
+    mate_start(2, 1)
+    attend_peers(3, 6)
+    y_forward(3, 2)
+    mate_start(2, 2)
+    mate_start(3, -1)
+    mate_start(3, 1)
+    attend_peers(6, groups)
     att_r[:, lane_at] = attend(lv)
-    mate_start(1, 2)
-    mate_wait(1)
+    mate_start(3, 2)
+    mate_wait(2)
 
     @pl.loop(1, groups)
     def _(k):
@@ -354,6 +381,7 @@
         at = pl.ds(pl.multiple_of(i * chunk, chunk), chunk)
         normed[at] = layer_norm(after[at]).astype(BF16)
 
+    mate_wait(3)
     edge = padded.shape[0] - rows
     edge = edge // 2
     piece = 256

time: 136 us -> 129 us (0.949)
  Pallas kernels: 129 us -> 123 us
    pallas_call x1, Pallas kernels: 129 us -> 123 us  [body(): pl.pallas_call(step_kernel, out_shape=jax.ShapeDtypeStruct((frames, level...]
where the time goes in v2:
time: 129 us
  Pallas kernels  123 us (95%)
  local copies, waits for them, and re-layouts  4.69 us (4%)
    pallas_call x1, Pallas kernels, body(): pl.pallas_call(step_kernel, out_shape=jax.ShapeDtypeStruct((frames, level...  123 us
    unnamed x1, local copies, waits for them, and re-layouts  3.86 us

profile of v2, /device:TPU:32, one launch (start us, length us, event | category | flops | bytes accessed | tf_op | source)
XLA Modules:
  0.0 128.7 jit_solution(2068040020139309114)
XLA Ops:
  0.7 0.7 convert_reduce_fusion
  1.4 0.1 reshape.11
  1.5 0.8 copy.12
  2.2 122.6 %shard_map.109 = bf16[1536,1024]{1,0:T(8,128)(2,1)} custom-call(f32[192,8]{1,0:T(8,128)} %bitcast.11, bf16[1,1024]{1,0:T(2,128)(2,1)} %fill_ref.1, bf16[5,1024]{1,0:T(8,128)(2,1)} %taps_ref.1, bf16[1024,1024]{1,0:T(8,128)(2,1)} %bitcast.9, bf16[3,32,128]{2,1,0:T(8,128)(2,1)} %wqkv_hbm.1, bf16[32,128]{1,0:T(8,128)(2,1)} %bitcast.12, ...), custom_call_target="tpu_custom_call" | custom-call | tf_op jit(solution)/shard_map/pallas_call | solution.py:500
  124.9 3.9 %copy.15 = bf16[1,1,1536,1024]{3,2,1,0:T(8,128)(2,1)} copy(bf16[1,1,1536,1024]{3,2,1,0:T(8,128)(2,1)} %bitcast.8) | data formatting | bytes 6291456

commit v3 on v1

v3 whole, which is shorter than its diff:
```python
import jax
import jax.numpy as jnp
from jax import lax
from jax.experimental import pallas as pl
from jax.experimental.pallas import tpu as pltpu
from jax.sharding import PartitionSpec as P

MESH = pl.DeviceIdType.MESH
BF16, F32 = jnp.bfloat16, jnp.float32

HEADS = 16
NZ, NY, NC = 4, 4, 2
NX, NL = 4, 2
LANES = 128
SENDS, ARRIVALS = 40, 92
Q, K, V, OUT, EXPAND, JOIN = range(6)


def layer_norm(values):
    centered = values - jnp.mean(values, axis=-1, keepdims=True)
    variance = jnp.mean(centered * centered, axis=-1, keepdims=True)
    return centered * lax.rsqrt(variance + 1e-05)


def step_kernel(
    sel_ref,
    fill_ref,
    taps_ref,
    table_hbm,
    wqkv_hbm,
    wout_hbm,
    wexp_hbm,
    wproj_hbm,
    head_hbm,
    out,
    table,
    head,
    weights,
    terms,
    partial,
    zsend,
    zrecv,
    own,
    normed,
    qkv_s,
    qkv_r,
    att_s,
    att_r,
    after,
    gated,
    halo,
    padded,
    active,
    final,
    probs,
    sums,
    load_sem,
    send_sem,
    recv_sem,
    att_send,
):
    groups = NX * NL
    rows, width = own.shape
    frames = rows * groups
    half = width // 2
    shard = weights.shape[3]

    dp = lax.axis_index("dp")
    lv = lax.axis_index("level")
    core = lax.rem(dp, NC)
    yy = lax.rem(dp // NC, NY)
    zh = dp // (NC * NY)
    xx, zl = lv // NL, lax.rem(lv, NL)
    zy = zh * NY + yy

    def level_of(dx, dz):
        return lax.rem(xx + dx + NX, NX) * NL + lax.rem(zl + dz, NL)

    def dp_of(dz, dy, dc):
        return (lax.rem(zh + dz + NZ, NZ) * NY + lax.rem(yy + dy + NY, NY)) * NC + lax.rem(core + dc, NC)

    x_up, x_down, z_mate = {"level": level_of(1, 0)}, {"level": level_of(-1, 0)}, {"level": level_of(0, 1)}
    z_up, z_down = {"dp": dp_of(1, 0, 0)}, {"dp": dp_of(-1, 0, 0)}
    y_up, y_down = {"dp": dp_of(0, 1, 0)}, {"dp": dp_of(0, -1, 0)}
    core_mate = {"dp": dp_of(0, 0, 1)}

    lane_at = pl.ds(pl.multiple_of(lv * LANES, LANES), LANES)
    loads = [
        pltpu.make_async_copy(table_hbm, table, load_sem.at[0]),
        pltpu.make_async_copy(wqkv_hbm, weights.at[zy, core, pl.ds(0, 3), :, lane_at], load_sem.at[1]),
        pltpu.make_async_copy(wout_hbm, weights.at[zy, core, 3, :, lane_at], load_sem.at[2]),
        pltpu.make_async_copy(wexp_hbm.at[:, pl.ds(0, width)], weights.at[zy, core, 4], load_sem.at[3]),
        pltpu.make_async_copy(wexp_hbm.at[:, pl.ds(width, width)], weights.at[zy, core, 5], load_sem.at[4]),
        pltpu.make_async_copy(wproj_hbm, weights.at[zy, core, 6], load_sem.at[5]),
        pltpu.make_async_copy(head_hbm, head, load_sem.at[6]),
    ]
    for load in loads:
        load.start()

    barrier = pltpu.get_barrier_semaphore()
    for k in range(1, groups):
        pl.semaphore_signal(barrier, inc=1, device_id={"level": level_of(k // NL, k % NL)}, device_id_type=MESH)
    for peer in (z_up, z_down, y_up, y_down, core_mate):
        pl.semaphore_signal(barrier, inc=1, device_id=peer, device_id_type=MESH)
    sent, arrivals = [], []

    def make(src, dst, device, out_sem, in_sem):
        return pltpu.make_async_remote_copy(
            src_ref=src, dst_ref=dst, send_sem=out_sem, recv_sem=in_sem, device_id=device, device_id_type=MESH
        )

    def arrival():
        arrivals.append(recv_sem.at[len(arrivals)])
        return arrivals[-1]

    def send(src, dst, device, in_sem):
        n = len(sent)
        if n >= SENDS:
            sent[n - SENDS].wait_send()
        copy = make(src, dst, device, send_sem.at[n % SENDS], in_sem)
        copy.start()
        sent.append(copy)

    def await_bytes(ref, in_sem):
        make(ref, ref, core_mate, send_sem.at[0], in_sem).wait_recv()

    codes = lax.broadcasted_iota(jnp.int32, (rows, table.shape[0]), 1).astype(F32)
    slots = lax.broadcasted_iota(jnp.int32, (rows, groups), 1)

    def term(dx, dz):
        dest = level_of(dx, dz)
        ids = jnp.sum(jnp.where(slots == dest, sel_ref[...], 0.0), axis=1, keepdims=True)
        onehot = jnp.where(ids == codes, 1.0, 0.0).astype(BF16)
        picked = jnp.dot(onehot, table[...], preferred_element_type=F32)
        terms[dest] = jnp.where(ids < 0.0, fill_ref[...].astype(F32), picked).astype(BF16)

    def col(d):
        return pl.ds(d * half, half)

    parts = ((1, pl.ds(0, rows)), (0, pl.ds(0, rows // 2)), (0, pl.ds(rows // 2, rows // 2)))

    def ring_send(step, p):
        dz, at = parts[p]
        ring[step, p] = arrival()
        for d in range(2):
            block = terms.at[level_of(NX - step if d == 0 else step, dz), at, col(d)]
            send(block, partial.at[d, step - 1, 1 - dz, at], x_up if d == 0 else x_down, ring[step, p])

    ring = {}
    loads[0].wait()

    @pl.loop(0, 4)
    def _(i):
        term(2 * lax.rem(i, 2) + NX - 1, 1 - i // 2)

    spans = (pl.ds(0, 1), pl.ds(1, 1), pl.ds(2, 1), pl.ds(3, 1), pl.ds(4, 2), pl.ds(6, 1))
    low, high = pl.ds(0, shard // 2), pl.ds(shard // 2, shard // 2)

    def place(dz, dy, g, part=None):
        at = lax.rem(zh + dz + NZ, NZ) * NY + lax.rem(yy + dy + NY, NY)
        if part is None:
            return weights.at[at, core, spans[g]]
        return weights.at[at, core, spans[g], part]

    znear, zfar, ynear, yfar, mate = {}, {}, {}, {}, {}

    def z_start(g):
        block = place(0, 0, g)
        znear[g] = arrival()
        send(block, block, z_up, znear[g])
        send(block, block, z_down, znear[g])

    def z_forward(g):
        await_bytes(weights.at[pl.ds(0, 2), core, spans[g]], znear[g])
        one, two = place(-1, 0, g, low), place(1, 0, g, high)
        zfar[g] = arrival()
        send(one, one, z_up, zfar[g])
        send(two, two, z_down, zfar[g])

    def z_last(g):
        await_bytes(weights.at[0, core, spans[g]], zfar[g])

    def y_start(g, dz):
        block = place(dz, 0, g)
        ynear[g, dz] = arrival()
        send(block, block, y_up, ynear[g, dz])
        send(block, block, y_down, ynear[g, dz])

    def y_forward(g, dz):
        await_bytes(weights.at[pl.ds(0, 2), core, spans[g]], ynear[g, dz])
        one, two = place(dz, -1, g, low), place(dz, 1, g, high)
        yfar[g, dz] = arrival()
        send(one, one, y_up, yfar[g, dz])
        send(two, two, y_down, yfar[g, dz])

    def mate_start(g, dz):
        await_bytes(weights.at[0, core, spans[g]], yfar[g, dz])
        plane = weights.at[pl.ds(lax.rem(zh + dz + NZ, NZ) * NY, NY), core, spans[g]]
        if g not in mate:
            mate[g] = arrival()
        send(plane, plane, core_mate, mate[g])

    def mate_wait(g):
        await_bytes(weights.at[:, core, spans[g]], mate[g])

    z_sem = arrival()

    def ring_next(step, p):
        dz, at = parts[p]
        await_bytes(partial.at[:, step - 1, 1 - dz, at], ring[step, p])
        for d in range(2):
            dest = level_of(2 * NX - step - 1 if d == 0 else step + 1, dz)
            total = terms[dest, at, col(d)].astype(F32) + partial[d, step - 1, 1 - dz, at].astype(F32)
            if step < NX - 1:
                terms[dest, at, col(d)] = total.astype(BF16)
            elif dz == 1:
                zsend[d] = total.astype(BF16)
                send(zsend.at[d], zrecv.at[d], z_mate, z_sem)
            else:
                own[at, col(d)] = total
        if step < NX - 1:
            ring_send(step + 1, p)

    pl.semaphore_wait(barrier, groups + 4)
    for load in loads[1:6]:
        load.wait()

    def columns_start(j, count):
        block = weights.at[zy, core, pl.ds(j, count), :, lane_at]
        sem = arrival()
        for k in range(1, groups):
            send(block, block, {"level": level_of(k // NL, k % NL)}, sem)
        return sem

    def columns_wait(j, count, sem):
        await_bytes(weights.at[zy, core, pl.ds(j, count), :, pl.ds(0, (groups - 1) * LANES)], sem)

    qkv_columns = columns_start(0, 3)
    ring_send(1, 0)
    ring_send(1, 1)
    y_start(EXPAND, 0)
    y_start(JOIN, 0)

    @pl.loop(0, 4)
    def _(i):
        term(2 + 2 * (i // 2), lax.rem(i + 1, 2))

    columns_wait(0, 3, qkv_columns)
    for g in (K, Q, V):
        z_start(g)
        y_start(g, 0)
    ring_next(1, 0)
    ring_send(1, 2)
    y_forward(K, 0)
    y_forward(Q, 0)
    z_forward(K)
    y_start(K, -1)
    y_start(K, 1)
    y_forward(V, 0)
    y_forward(EXPAND, 0)
    y_forward(JOIN, 0)
    z_forward(Q)
    y_start(Q, -1)
    y_start(Q, 1)
    ring_next(2, 0)
    ring_next(1, 1)
    z_forward(V)
    y_start(V, -1)
    y_start(V, 1)
    ring_next(1, 2)
    z_start(EXPAND)
    out_columns = columns_start(3, 1)
    mate_start(K, 0)
    mate_start(Q, 0)
    mate_start(V, 0)
    z_last(K)
    y_start(K, 2)
    z_last(Q)
    y_start(Q, 2)
    y_forward(K, -1)
    y_forward(K, 1)
    z_last(V)
    y_start(V, 2)
    ring_next(3, 0)
    ring_next(2, 1)
    y_forward(Q, -1)
    y_forward(Q, 1)
    ring_next(2, 2)
    z_forward(EXPAND)
    columns_wait(3, 1, out_columns)
    z_start(OUT)
    z_start(JOIN)
    y_forward(V, -1)
    y_forward(V, 1)
    y_forward(K, 2)
    y_forward(Q, 2)
    ring_next(3, 1)
    y_forward(V, 2)
    y_start(EXPAND, -1)
    y_start(EXPAND, 1)
    y_start(OUT, 0)
    mate_start(K, -1)
    mate_start(K, 1)
    mate_start(Q, -1)
    mate_start(Q, 1)
    ring_next(3, 2)
    mate_start(V, -1)
    mate_start(V, 1)
    mate_start(K, 2)
    mate_start(Q, 2)
    mate_start(V, 2)
    await_bytes(zrecv, z_sem)
    for d in range(2):
        own[:, col(d)] += zrecv[d].astype(F32)

    chunk = rows // 2

    @pl.loop(0, rows // chunk)
    def _(i):
        at = pl.ds(pl.multiple_of(i * chunk, chunk), chunk)
        normed[at] = layer_norm(own[at]).astype(BF16)

    mate_wait(K)

    def weight(j, start, size):
        return weights[:, :, j, :, pl.ds(start, size)].reshape(width, size)

    def project(j):
        size = half
        for h in range(width // size):
            product = jnp.dot(normed[...], weight(j, h * size, size), preferred_element_type=F32)
            for i in range(size // LANES):
                qkv_s[h * (size // LANES) + i, j] = product[:, i * LANES : (i + 1) * LANES].astype(BF16)

    def exchange(j, count):
        sem = arrival()
        for k in (4, 5, 2, 3, 6, 7, 1):
            dest = level_of(k // NL, k % NL)
            send(qkv_s.at[dest, pl.ds(j, count)], qkv_r.at[lv, pl.ds(j, count)], {"level": dest}, sem)
        qkv_r[lv, pl.ds(j, count)] = qkv_s[lv, pl.ds(j, count)]
        return sem

    project(1)
    mate_wait(Q)
    project(0)
    qk_sem = exchange(0, 2)
    mate_wait(V)
    project(2)
    v_sem = exchange(2, 1)
    z_last(EXPAND)
    y_start(EXPAND, 2)
    z_forward(OUT)
    y_start(OUT, -1)
    y_start(OUT, 1)
    z_forward(JOIN)
    y_start(JOIN, -1)
    y_start(JOIN, 1)
    mate_start(EXPAND, 0)
    mate_start(JOIN, 0)
    y_forward(EXPAND, -1)
    y_forward(EXPAND, 1)
    y_forward(OUT, 0)
    y_forward(EXPAND, 2)
    await_bytes(qkv_r.at[pl.ds(0, groups - 1), pl.ds(0, 2)], qk_sem)

    head_dim = width // HEADS
    att_sem = arrival()

    heads = LANES // head_dim

    def source(k):
        return level_of(NX - k // NL, NL - lax.rem(k, NL))

    def lane_head():
        return lax.broadcasted_iota(jnp.int32, (rows, LANES), 1) // head_dim

    def score(k):
        src = source(k)
        query = qkv_r[src, 0].astype(F32) * head_dim ** (-0.5)
        keys = qkv_r[:, 1].reshape(frames, LANES)
        total = jnp.zeros((rows, LANES), F32)
        for h in range(heads):
            masked = jnp.where(lane_head() == h, query, 0.0).astype(BF16)
            scores = lax.dot_general(masked, keys, (((1,), (1,)), ((), ())), preferred_element_type=F32)
            grown = jnp.exp(scores - jnp.max(scores, axis=-1, keepdims=True))
            probs[src, h] = grown.astype(BF16)
            total = jnp.where(lane_head() == h, jnp.sum(grown, axis=-1, keepdims=True), total)
        sums[src] = total

    def mix(k):
        src = source(k)
        values = qkv_r[:, 2].reshape(frames, LANES)
        merged = jnp.dot(probs[src, 0], values, preferred_element_type=F32)
        for h in range(1, heads):
            merged = jnp.where(lane_head() == h, jnp.dot(probs[src, h], values, preferred_element_type=F32), merged)
        return (merged / sums[src]).astype(BF16)

    def att_copy(k):
        src = source(k)
        return src, make(att_s.at[src], att_r.at[:, lane_at], {"level": src}, att_send, att_sem)

    def mix_send(k):
        src, copy = att_copy(k)
        att_s[src] = mix(k)
        copy.start()

    @pl.loop(1, 4)
    def _(k):
        score(k)

    z_last(OUT)
    y_start(OUT, 2)
    z_last(JOIN)
    y_start(JOIN, 2)
    await_bytes(qkv_r.at[pl.ds(0, groups - 1), 2], v_sem)

    @pl.loop(1, 4)
    def _(k):
        score(k + 3)
        mix_send(k)

    y_forward(OUT, -1)
    y_forward(OUT, 1)
    y_forward(OUT, 2)
    mate_start(EXPAND, -1)
    mate_start(EXPAND, 1)
    score(7)
    mix_send(4)
    score(0)
    mix_send(5)

    @pl.loop(6, groups)
    def _(k):
        mix_send(k)

    y_forward(JOIN, -1)
    y_forward(JOIN, 1)
    y_forward(JOIN, 2)
    mate_start(OUT, 0)
    mate_start(OUT, -1)
    mate_start(OUT, 1)
    att_r[:, lane_at] = mix(0)
    mate_start(EXPAND, 2)
    mate_start(OUT, 2)
    await_bytes(att_r.at[:, pl.ds(0, (groups - 1) * LANES)], att_sem)
    mate_wait(OUT)

    attended = lax.dot_general(
        att_r[...], weight(3, 0, width), (((1,), (1,)), ((), ())), preferred_element_type=F32
    )
    after[...] = own[...] + attended

    @pl.loop(0, rows // chunk)
    def _(i):
        at = pl.ds(pl.multiple_of(i * chunk, chunk), chunk)
        normed[at] = layer_norm(after[at]).astype(BF16)

    mate_start(JOIN, -1)
    mate_start(JOIN, 1)
    mate_wait(EXPAND)
    edge = padded.shape[0] - rows
    edge = edge // 2
    piece = 256
    for h in range(width // piece):
        linear = jnp.dot(normed[...], weight(4, h * piece, piece), preferred_element_type=F32)
        gate = jnp.dot(normed[...], weight(5, h * piece, piece), preferred_element_type=F32)
        value = (linear * jax.nn.sigmoid(gate)).astype(BF16)
        gated[:, pl.ds(h * piece, piece)] = value
        padded[pl.ds(edge, rows), pl.ds(h * piece, piece)] = value.astype(F32)
    tile = halo.shape[1]
    after_me, before_me = lax.rem(lv + 1, groups), lax.rem(lv + groups - 1, groups)
    mate_start(JOIN, 2)
    edge_sem = arrival()
    send(gated.at[pl.ds(rows - tile, tile)], halo.at[0], {"level": after_me}, edge_sem)
    send(gated.at[pl.ds(0, tile)], halo.at[1], {"level": before_me}, edge_sem)

    taps = taps_ref.shape[0]
    reach = taps // 2

    def convolve(start, count):
        conv = jnp.zeros((count, width), F32)
        for t in range(taps):
            conv = conv + padded[pl.ds(edge + start + t - reach, count)] * taps_ref[pl.ds(t, 1)].astype(F32)
        active[pl.ds(start, count)] = (conv * jax.nn.sigmoid(conv)).astype(BF16)

    for start in range(tile, rows - tile, 32):
        convolve(start, 32)
    await_bytes(halo, edge_sem)
    padded[pl.ds(0, edge)] = jnp.where(lv > 0, halo[0, pl.ds(tile - edge, edge)].astype(F32), 0.0)
    padded[pl.ds(edge + rows, edge)] = jnp.where(lv < groups - 1, halo[1, pl.ds(0, edge)].astype(F32), 0.0)
    convolve(0, tile)
    convolve(rows - tile, tile)
    mate_wait(JOIN)
    after[...] += jnp.dot(active[...], weight(6, 0, width), preferred_element_type=F32)

    @pl.loop(0, rows // chunk)
    def _(i):
        at = pl.ds(pl.multiple_of(i * chunk, chunk), chunk)
        final[lv, at] = layer_norm(after[at]).astype(BF16)

    def logits(block):
        at = pl.ds(pl.multiple_of(block * rows, rows), rows)
        for h in range(2):
            product = jnp.dot(final[block], head[:, col(h)], preferred_element_type=F32)
            out[at, col(h)] = product.astype(BF16)

    mine = final.at[lv]
    side_sem, mate_sem, far_sem, last_sem = arrival(), arrival(), arrival(), arrival()
    down_sem, up_sem = arrival(), arrival()
    send(mine, mine, x_up, side_sem)
    send(mine, mine, x_down, side_sem)
    send(mine, mine, z_mate, mate_sem)
    top, bottom = pl.ds(0, rows // 2), pl.ds(rows // 2, rows // 2)
    loads[6].wait()
    logits(lv)
    await_bytes(final.at[pl.ds(0, 2)], side_sem)
    one, two = final.at[level_of(-1, 0), top], final.at[level_of(1, 0), bottom]
    send(one, one, x_up, far_sem)
    send(two, two, x_down, far_sem)
    await_bytes(final.at[0], mate_sem)
    mate_block = final.at[level_of(0, 1)]
    send(mate_block, mate_block, x_up, down_sem)
    send(mate_block, mate_block, x_down, up_sem)
    logits(level_of(-1, 0))
    logits(level_of(1, 0))
    await_bytes(final.at[0], far_sem)
    opposite = final.at[level_of(2, 0)]
    send(opposite, opposite, z_mate, last_sem)
    logits(level_of(0, 1))
    logits(level_of(2, 0))
    await_bytes(final.at[0], down_sem)
    logits(level_of(-1, 1))
    await_bytes(final.at[0], up_sem)
    logits(level_of(1, 1))
    await_bytes(final.at[0], last_sem)
    logits(level_of(2, 1))

    for copy in sent[-SENDS:]:
        copy.wait_send()
    await_send = make(
        att_s.at[pl.ds(0, groups - 1)], att_s.at[pl.ds(0, groups - 1)], core_mate, att_send, recv_sem.at[0]
    )
    await_send.wait_send()


def body(
    token_ids,
    decoded_mask,
    levels_done,
    code_tables,
    mask_vectors,
    w_qkv,
    w_out,
    w_expand,
    w_depth,
    w_project,
    level_heads,
):
    frames = token_ids.shape[2]
    width = code_tables.shape[2]
    groups = lax.axis_size("level")
    level = lax.axis_index("level")
    rows = frames // groups
    done = levels_done[0]
    use_token = (level < done) | (level == done) & (decoded_mask[0, 0] == 1)
    sel = jnp.where(use_token, token_ids[0, 0], -1).astype(F32).reshape(groups, rows).T
    shard = w_project.shape[0]
    tile, edge = 16, 8
    vmem = pl.BlockSpec(memory_space=pltpu.VMEM)
    hbm = pl.BlockSpec(memory_space=pl.ANY)
    logits = pl.pallas_call(
        step_kernel,
        out_shape=pltpu.VMEM((frames, level_heads.shape[2]), BF16),
        in_specs=[vmem] * 3 + [hbm] * 6,
        out_specs=vmem,
        scratch_shapes=[
            pltpu.VMEM(code_tables.shape[1:], BF16),
            pltpu.VMEM(level_heads.shape[1:], BF16),
            pltpu.VMEM((NZ * NY, NC, 7, shard, width), BF16),
            pltpu.VMEM((groups, rows, width), BF16),
            pltpu.VMEM((2, NX - 1, 2, rows, width // 2), BF16),
            pltpu.VMEM((2, rows, width // 2), BF16),
            pltpu.VMEM((2, rows, width // 2), BF16),
            pltpu.VMEM((rows, width), F32),
            pltpu.VMEM((rows, width), BF16),
            pltpu.VMEM((groups, 3, rows, LANES), BF16),
            pltpu.VMEM((groups, 3, rows, LANES), BF16),
            pltpu.VMEM((groups, rows, LANES), BF16),
            pltpu.VMEM((rows, width), BF16),
            pltpu.VMEM((rows, width), F32),
            pltpu.VMEM((rows, width), BF16),
            pltpu.VMEM((2, tile, width), BF16),
            pltpu.VMEM((rows + 2 * edge, width), F32),
            pltpu.VMEM((rows, width), BF16),
            pltpu.VMEM((groups, rows, width), BF16),
            pltpu.VMEM((groups, LANES * HEADS // width, rows, frames), BF16),
            pltpu.VMEM((groups, rows, LANES), F32),
            pltpu.SemaphoreType.DMA((7,)),
            pltpu.SemaphoreType.DMA((SENDS,)),
            pltpu.SemaphoreType.DMA((ARRIVALS,)),
            pltpu.SemaphoreType.DMA,
        ],
        compiler_params=pltpu.CompilerParams(
            collective_id=0, has_side_effects=True, vmem_limit_bytes=60 * 1024 * 1024
        ),
    )(
        sel,
        mask_vectors,
        w_depth,
        code_tables[0],
        w_qkv,
        w_out.T,
        w_expand,
        w_project,
        level_heads[0],
    )
    return logits[None, None]


def solution(mesh):
    return jax.shard_map(
        body,
        mesh=mesh,
        in_specs=(
            P("dp", "level", None),
            P("dp", "level", None),
            P("dp"),
            P("level", None, None),
            P("level", None),
            P(None, "dp", "level"),
            P("level", "dp"),
            P("dp", None),
            P(),
            P("dp", None),
            P("level", None, None),
        ),
        out_specs=P("dp", "level", None, None),
        check_vma=False,
    )
```

time: 136 us -> 118 us (0.87)
  Pallas kernels: 129 us -> 113 us
  local copies, waits for them, and re-layouts: 4.69 us -> 2.5 us
    pallas_call x1, Pallas kernels: 129 us -> 113 us  [body(): pl.pallas_call(step_kernel, out_shape=pltpu.VMEM((frames, level_heads.sha...]
    unnamed x1, local copies, waits for them, and re-layouts: 3.86 us -> 1.67 us
where the time goes in v3:
time: 118 us; the launch traced here: 117 us
  Pallas kernels  113 us (96%)
  local copies, waits for them, and re-layouts  2.5 us (2%)
    pallas_call x1, Pallas kernels, body(): pl.pallas_call(step_kernel, out_shape=pltpu.VMEM((frames, level_heads.sha...  113 us

profile of v3, /device:TPU:32, one launch (start us, length us, event | category | flops | bytes accessed | tf_op | source)
XLA Modules:
  0.0 117.3 jit_solution(15039088772558051409)
XLA Ops:
  0.7 0.7 convert_reduce_fusion
  1.4 0.1 reshape.11
  1.5 0.8 copy.12
  2.2 113.4 %shard_map.109 = bf16[1536,1024]{1,0:T(8,128)(2,1)S(1)} custom-call(f32[192,8]{1,0:T(8,128)} %bitcast.11, bf16[1,1024]{1,0:T(2,128)(2,1)} %fill_ref.1, bf16[5,1024]{1,0:T(8,128)(2,1)} %taps_ref.1, bf16[1024,1024]{1,0:T(8,128)(2,1)} %bitcast.9, bf16[3,32,128]{2,1,0:T(8,128)(2,1)} %wqkv_hbm.1, bf16[32,128]{1,0:T(8,128)(2,1)} %bitcast.12, ...), custom_call_target="tpu_custom_call" | custom-call | tf_op jit(solution)/shard_map/pallas_call | solution.py:571
  115.6 1.7 %copy.14 = bf16[1,1,1536,1024]{3,2,1,0:T(8,128)(2,1)} copy(bf16[1,1,1536,1024]{3,2,1,0:T(8,128)(2,1)S(1)} %bitcast.8) | data formatting | bytes 6291456

commit v4 on v3

--- a/solution.py
+++ b/solution.py
@@ -12,7 +12,8 @@
 NZ, NY, NC = 4, 4, 2
 NX, NL = 4, 2
 LANES = 128
-SENDS, ARRIVALS = 40, 92
+EDGE = 16
+SENDS, ARRIVALS = 40, 104
 Q, K, V, OUT, EXPAND, JOIN = range(6)
 
 
@@ -23,7 +24,9 @@
 
 
 def step_kernel(
-    sel_ref,
+    ids_ref,
+    mask_ref,
+    done_ref,
     fill_ref,
     taps_ref,
     table_hbm,
@@ -35,6 +38,7 @@
     out,
     table,
     head,
+    id_rows,
     weights,
     terms,
     partial,
@@ -47,8 +51,6 @@
     att_s,
     att_r,
     after,
-    gated,
-    halo,
     padded,
     active,
     final,
@@ -60,8 +62,11 @@
     att_send,
 ):
     groups = NX * NL
-    rows, width = own.shape
+    rows, width = active.shape
     frames = rows * groups
+    wide = own.shape[0]
+    edge = (wide - rows) // 2
+    inner = pl.ds(edge, rows)
     half = width // 2
     shard = weights.shape[3]
 
@@ -124,15 +129,22 @@
     def await_bytes(ref, in_sem):
         make(ref, ref, core_mate, send_sem.at[0], in_sem).wait_recv()
 
-    codes = lax.broadcasted_iota(jnp.int32, (rows, table.shape[0]), 1).astype(F32)
-    slots = lax.broadcasted_iota(jnp.int32, (rows, groups), 1)
+    done = done_ref[0]
+    flags = jnp.where(lv < done, 1, jnp.where(lv == done, mask_ref[...], 0))
+    picks = jnp.where(flags == 1, ids_ref[...], -1).astype(F32)
+    for i in range(frames // LANES):
+        part = jnp.broadcast_to(picks[:, i * LANES : (i + 1) * LANES], (LANES, LANES))
+        id_rows[pl.ds(i * LANES, LANES)] = part.T
+    codes = lax.broadcasted_iota(jnp.int32, (rows, LANES), 1).astype(F32)
+    tiles = table.shape[0] // LANES
 
     def term(dx, dz):
         dest = level_of(dx, dz)
-        ids = jnp.sum(jnp.where(slots == dest, sel_ref[...], 0.0), axis=1, keepdims=True)
-        onehot = jnp.where(ids == codes, 1.0, 0.0).astype(BF16)
+        ids = id_rows[pl.ds(pl.multiple_of(dest * rows, rows), rows)]
+        onehot = jnp.concatenate([jnp.where(ids == codes + i * LANES, 1.0, 0.0).astype(BF16) for i in range(tiles)], axis=1)
         picked = jnp.dot(onehot, table[...], preferred_element_type=F32)
-        terms[dest] = jnp.where(ids < 0.0, fill_ref[...].astype(F32), picked).astype(BF16)
+        masked = jnp.concatenate([ids] * (width // LANES), axis=1) < 0.0
+        terms[dest] = jnp.where(masked, fill_ref[...].astype(F32), picked).astype(BF16)
 
     def col(d):
         return pl.ds(d * half, half)
@@ -156,11 +168,21 @@
     spans = (pl.ds(0, 1), pl.ds(1, 1), pl.ds(2, 1), pl.ds(3, 1), pl.ds(4, 2), pl.ds(6, 1))
     low, high = pl.ds(0, shard // 2), pl.ds(shard // 2, shard // 2)
 
-    def place(dz, dy, g, part=None):
+    quarter = width // NX
+    all_rows, all_lanes = pl.ds(0, shard), pl.ds(0, width)
+
+    def quarter_at(dx):
+        return pl.ds(pl.multiple_of(lax.rem(xx + dx + NX, NX) * quarter, LANES), quarter)
+
+    def lanes(g):
+        return quarter_at(0) if g == JOIN else all_lanes
+
+    def blocks(at, g, part=all_rows):
+        return weights.at[at, core, spans[g], part, lanes(g)]
+
+    def place(dz, dy, g, part=all_rows):
         at = lax.rem(zh + dz + NZ, NZ) * NY + lax.rem(yy + dy + NY, NY)
-        if part is None:
-            return weights.at[at, core, spans[g]]
-        return weights.at[at, core, spans[g], part]
+        return blocks(at, g, part)
 
     znear, zfar, ynear, yfar, mate = {}, {}, {}, {}, {}
 
@@ -171,14 +193,14 @@
         send(block, block, z_down, znear[g])
 
     def z_forward(g):
-        await_bytes(weights.at[pl.ds(0, 2), core, spans[g]], znear[g])
+        await_bytes(blocks(pl.ds(0, 2), g), znear[g])
         one, two = place(-1, 0, g, low), place(1, 0, g, high)
         zfar[g] = arrival()
         send(one, one, z_up, zfar[g])
         send(two, two, z_down, zfar[g])
 
     def z_last(g):
-        await_bytes(weights.at[0, core, spans[g]], zfar[g])
+        await_bytes(blocks(0, g), zfar[g])
 
     def y_start(g, dz):
         block = place(dz, 0, g)
@@ -187,18 +209,42 @@
         send(block, block, y_down, ynear[g, dz])
 
     def y_forward(g, dz):
-        await_bytes(weights.at[pl.ds(0, 2), core, spans[g]], ynear[g, dz])
+        await_bytes(blocks(pl.ds(0, 2), g), ynear[g, dz])
         one, two = place(dz, -1, g, low), place(dz, 1, g, high)
         yfar[g, dz] = arrival()
         send(one, one, y_up, yfar[g, dz])
         send(two, two, y_down, yfar[g, dz])
 
     def mate_start(g, dz):
-        await_bytes(weights.at[0, core, spans[g]], yfar[g, dz])
+        await_bytes(blocks(0, g), yfar[g, dz])
         plane = weights.at[pl.ds(lax.rem(zh + dz + NZ, NZ) * NY, NY), core, spans[g]]
         if g not in mate:
             mate[g] = arrival()
         send(plane, plane, core_mate, mate[g])
+
+    x_sems = []
+
+    def x_start():
+        for dz in (0, -1, 1, 2):
+            await_bytes(blocks(0, JOIN), yfar[JOIN, dz])
+        x_sems.extend([arrival(), arrival()])
+        block = weights.at[:, core, 6, :, quarter_at(0)]
+        send(block, block, x_up, x_sems[0])
+        send(block, block, x_down, x_sems[0])
+
+    def x_forward():
+        half_at = NZ * NY // 2
+        await_bytes(weights.at[:, core, 6, :, pl.ds(0, 2 * quarter)], x_sems[0])
+        one = weights.at[pl.ds(0, half_at), core, 6, :, quarter_at(-1)]
+        two = weights.at[pl.ds(half_at, half_at), core, 6, :, quarter_at(1)]
+        send(one, one, x_up, x_sems[1])
+        send(two, two, x_down, x_sems[1])
+
+    def x_mate():
+        await_bytes(weights.at[:, core, 6, :, pl.ds(0, quarter)], x_sems[1])
+        mate[JOIN] = arrival()
+        block = weights.at[:, core, 6]
+        send(block, block, core_mate, mate[JOIN])
 
     def mate_wait(g):
         await_bytes(weights.at[:, core, spans[g]], mate[g])
@@ -217,7 +263,7 @@
                 zsend[d] = total.astype(BF16)
                 send(zsend.at[d], zrecv.at[d], z_mate, z_sem)
             else:
-                own[at, col(d)] = total
+                own[pl.ds(edge + at.start, at.size), col(d)] = total
         if step < NX - 1:
             ring_send(step + 1, p)
 
@@ -237,6 +283,7 @@
 
     qkv_columns = columns_start(0, 3)
     ring_send(1, 0)
+    out_columns = columns_start(3, 1)
     ring_send(1, 1)
     y_start(EXPAND, 0)
     y_start(JOIN, 0)
@@ -249,6 +296,7 @@
     for g in (K, Q, V):
         z_start(g)
         y_start(g, 0)
+    z_start(JOIN)
     ring_next(1, 0)
     ring_send(1, 2)
     y_forward(K, 0)
@@ -257,7 +305,6 @@
     y_start(K, -1)
     y_start(K, 1)
     y_forward(V, 0)
-    y_forward(EXPAND, 0)
     y_forward(JOIN, 0)
     z_forward(Q)
     y_start(Q, -1)
@@ -267,9 +314,13 @@
     z_forward(V)
     y_start(V, -1)
     y_start(V, 1)
+    z_forward(JOIN)
+    y_start(JOIN, -1)
+    y_start(JOIN, 1)
     ring_next(1, 2)
+    columns_wait(3, 1, out_columns)
+    z_start(OUT)
     z_start(EXPAND)
-    out_columns = columns_start(3, 1)
     mate_start(K, 0)
     mate_start(Q, 0)
     mate_start(V, 0)
@@ -281,43 +332,49 @@
     y_forward(K, 1)
     z_last(V)
     y_start(V, 2)
+    z_last(JOIN)
+    y_start(JOIN, 2)
     ring_next(3, 0)
     ring_next(2, 1)
     y_forward(Q, -1)
     y_forward(Q, 1)
     ring_next(2, 2)
-    z_forward(EXPAND)
-    columns_wait(3, 1, out_columns)
-    z_start(OUT)
-    z_start(JOIN)
+    z_forward(OUT)
     y_forward(V, -1)
     y_forward(V, 1)
+    y_forward(JOIN, -1)
+    y_forward(JOIN, 1)
     y_forward(K, 2)
     y_forward(Q, 2)
     ring_next(3, 1)
     y_forward(V, 2)
-    y_start(EXPAND, -1)
-    y_start(EXPAND, 1)
-    y_start(OUT, 0)
+    y_forward(JOIN, 2)
+    for dz in (0, -1, 1):
+        y_start(OUT, dz)
+    y_forward(EXPAND, 0)
     mate_start(K, -1)
     mate_start(K, 1)
     mate_start(Q, -1)
     mate_start(Q, 1)
     ring_next(3, 2)
+    x_start()
     mate_start(V, -1)
     mate_start(V, 1)
     mate_start(K, 2)
     mate_start(Q, 2)
     mate_start(V, 2)
+    z_forward(EXPAND)
+    y_start(EXPAND, -1)
+    y_start(EXPAND, 1)
     await_bytes(zrecv, z_sem)
     for d in range(2):
-        own[:, col(d)] += zrecv[d].astype(F32)
+        own[inner, col(d)] += zrecv[d].astype(F32)
 
     chunk = rows // 2
 
     @pl.loop(0, rows // chunk)
     def _(i):
-        at = pl.ds(pl.multiple_of(i * chunk, chunk), chunk)
+        at = pl.ds(pl.multiple_of(edge + i * chunk, 16), chunk)
         normed[at] = layer_norm(own[at]).astype(BF16)
 
     mate_wait(K)
@@ -328,44 +385,49 @@
     def project(j):
         size = half
         for h in range(width // size):
-            product = jnp.dot(normed[...], weight(j, h * size, size), preferred_element_type=F32)
+            product = jnp.dot(normed[inner], weight(j, h * size, size), preferred_element_type=F32)
             for i in range(size // LANES):
                 qkv_s[h * (size // LANES) + i, j] = product[:, i * LANES : (i + 1) * LANES].astype(BF16)
 
-    def exchange(j, count):
-        sem = arrival()
-        for k in (4, 5, 2, 3, 6, 7, 1):
+    def exchange(j, sems):
+        for i in range(1, groups):
+            k = 3 * i % groups
             dest = level_of(k // NL, k % NL)
-            send(qkv_s.at[dest, pl.ds(j, count)], qkv_r.at[lv, pl.ds(j, count)], {"level": dest}, sem)
-        qkv_r[lv, pl.ds(j, count)] = qkv_s[lv, pl.ds(j, count)]
-        return sem
-
+            send(qkv_s.at[dest, j], qkv_r.at[lv, j], {"level": dest}, sems[k % len(sems)])
+        qkv_r[lv, j] = qkv_s[lv, j]
+
+    def level_of_index(at):
+        return lax.rem(at + groups, groups)
+
+    k_sem = arrival()
     project(1)
+    exchange(1, (k_sem,))
     mate_wait(Q)
     project(0)
-    qk_sem = exchange(0, 2)
+    q_base = len(arrivals)
+    exchange(0, [arrival() for _ in range(groups)])
     mate_wait(V)
     project(2)
-    v_sem = exchange(2, 1)
+    v_sem = arrival()
+    exchange(2, (v_sem,))
+    side = (level_of_index(lv + 1), level_of_index(lv - 1))
+    edge_sem = arrival()
+    send(own.at[pl.ds(rows, edge)], own.at[pl.ds(0, edge)], {"level": side[0]}, edge_sem)
+    send(own.at[pl.ds(edge, edge)], own.at[pl.ds(edge + rows, edge)], {"level": side[1]}, edge_sem)
+    z_last(OUT)
+    y_start(OUT, 2)
+    x_forward()
+    for dz in (0, -1, 1):
+        y_forward(OUT, dz)
+    mate_start(EXPAND, 0)
     z_last(EXPAND)
     y_start(EXPAND, 2)
-    z_forward(OUT)
-    y_start(OUT, -1)
-    y_start(OUT, 1)
-    z_forward(JOIN)
-    y_start(JOIN, -1)
-    y_start(JOIN, 1)
-    mate_start(EXPAND, 0)
-    mate_start(JOIN, 0)
     y_forward(EXPAND, -1)
     y_forward(EXPAND, 1)
-    y_forward(OUT, 0)
-    y_forward(EXPAND, 2)
-    await_bytes(qkv_r.at[pl.ds(0, groups - 1), pl.ds(0, 2)], qk_sem)
+    await_bytes(qkv_r.at[pl.ds(0, groups - 1), 1], k_sem)
 
     head_dim = width // HEADS
-    att_sem = arrival()
-
+    att_sem, att_low, att_high = arrival(), arrival(), arrival()
     heads = LANES // head_dim
 
     def source(k):
@@ -395,54 +457,65 @@
             merged = jnp.where(lane_head() == h, jnp.dot(probs[src, h], values, preferred_element_type=F32), merged)
         return (merged / sums[src]).astype(BF16)
 
-    def att_copy(k):
+    def send_edges(src, out_low, out_high):
+        block = att_s.at[src]
+        for rows_at, lands, to, out_sem, in_sem in (
+            (pl.ds(rows - edge, edge), pl.ds(0, edge), level_of_index(src + 1), out_low, att_low),
+            (pl.ds(0, edge), pl.ds(edge + rows, edge), level_of_index(src - 1), out_high, att_high),
+        ):
+
+            @pl.when(to != lv)
+            def _():
+                make(block.at[rows_at], att_r.at[lands, lane_at], {"level": to}, out_sem, in_sem).start()
+
+            @pl.when(to == lv)
+            def _():
+                att_r[lands, lane_at] = att_s[src, rows_at]
+
+    def mix_send(k):
         src = source(k)
-        return src, make(att_s.at[src], att_r.at[:, lane_at], {"level": src}, att_send, att_sem)
-
-    def mix_send(k):
-        src, copy = att_copy(k)
         att_s[src] = mix(k)
-        copy.start()
-
-    @pl.loop(1, 4)
-    def _(k):
-        score(k)
-
-    z_last(OUT)
-    y_start(OUT, 2)
-    z_last(JOIN)
-    y_start(JOIN, 2)
+        make(att_s.at[src], att_r.at[inner, lane_at], {"level": src}, att_send.at[0], att_sem).start()
+        send_edges(src, att_send.at[1], att_send.at[2])
+
+    def scores_of(first, last):
+        @pl.loop(first, last)
+        def _(i):
+            k = lax.rem(3 * i, groups)
+            src = source(k)
+            make(qkv_s.at[src, 0], qkv_r.at[src, 0], {"level": src}, send_sem.at[0], recv_sem.at[q_base + k]).wait_recv()
+            score(k)
+
+    def mixes_of(first, last):
+        @pl.loop(first, last)
+        def _(i):
+            mix_send(lax.rem(3 * i, groups))
+
+    score(0)
+    scores_of(1, 3)
+    y_forward(OUT, 2)
+    mate_start(OUT, 0)
+    scores_of(3, 5)
+    mate_start(OUT, -1)
+    mate_start(OUT, 1)
+    scores_of(5, groups)
+    y_forward(EXPAND, 2)
     await_bytes(qkv_r.at[pl.ds(0, groups - 1), 2], v_sem)
-
-    @pl.loop(1, 4)
-    def _(k):
-        score(k + 3)
-        mix_send(k)
-
-    y_forward(OUT, -1)
-    y_forward(OUT, 1)
-    y_forward(OUT, 2)
+    mixes_of(1, 4)
+    mate_start(OUT, 2)
     mate_start(EXPAND, -1)
     mate_start(EXPAND, 1)
-    score(7)
-    mix_send(4)
-    score(0)
-    mix_send(5)
-
-    @pl.loop(6, groups)
-    def _(k):
-        mix_send(k)
-
-    y_forward(JOIN, -1)
-    y_forward(JOIN, 1)
-    y_forward(JOIN, 2)
-    mate_start(OUT, 0)
-    mate_start(OUT, -1)
-    mate_start(OUT, 1)
-    att_r[:, lane_at] = mix(0)
+    x_mate()
+    mixes_of(4, groups)
+    att_s[lv] = mix(0)
+    send_edges(lv, att_send.at[1], att_send.at[2])
+    att_r[inner, lane_at] = att_s[lv]
     mate_start(EXPAND, 2)
-    mate_start(OUT, 2)
-    await_bytes(att_r.at[:, pl.ds(0, (groups - 1) * LANES)], att_sem)
+    others = pl.ds(0, (groups - 1) * LANES)
+    await_bytes(att_r.at[inner, others], att_sem)
+    await_bytes(att_r.at[pl.ds(0, edge), others], att_low)
+    await_bytes(att_r.at[pl.ds(0, edge), others], att_high)
+    await_bytes(own.at[pl.ds(0, 2 * edge)], edge_sem)
     mate_wait(OUT)
 
     attended = lax.dot_general(
@@ -450,29 +523,22 @@
     )
     after[...] = own[...] + attended
 
-    @pl.loop(0, rows // chunk)
+    part = wide // 2
+
+    @pl.loop(0, wide // part)
     def _(i):
-        at = pl.ds(pl.multiple_of(i * chunk, chunk), chunk)
+        at = pl.ds(pl.multiple_of(i * part, 16), part)
         normed[at] = layer_norm(after[at]).astype(BF16)
 
-    mate_start(JOIN, -1)
-    mate_start(JOIN, 1)
     mate_wait(EXPAND)
-    edge = padded.shape[0] - rows
-    edge = edge // 2
     piece = 256
     for h in range(width // piece):
+        at = pl.ds(h * piece, piece)
         linear = jnp.dot(normed[...], weight(4, h * piece, piece), preferred_element_type=F32)
         gate = jnp.dot(normed[...], weight(5, h * piece, piece), preferred_element_type=F32)
-        value = (linear * jax.nn.sigmoid(gate)).astype(BF16)
-        gated[:, pl.ds(h * piece, piece)] = value
-        padded[pl.ds(edge, rows), pl.ds(h * piece, piece)] = value.astype(F32)
-    tile = halo.shape[1]
-    after_me, before_me = lax.rem(lv + 1, groups), lax.rem(lv + groups - 1, groups)
-    mate_start(JOIN, 2)
-    edge_sem = arrival()
-    send(gated.at[pl.ds(rows - tile, tile)], halo.at[0], {"level": after_me}, edge_sem)
-    send(gated.at[pl.ds(0, tile)], halo.at[1], {"level": before_me}, edge_sem)
+        padded[:, at] = (linear * jax.nn.sigmoid(gate)).astype(BF16).astype(F32)
+    padded[pl.ds(0, edge)] = jnp.where(lv > 0, padded[pl.ds(0, edge)], 0.0)
+    padded[pl.ds(edge + rows, edge)] = jnp.where(lv < groups - 1, padded[pl.ds(edge + rows, edge)], 0.0)
 
     taps = taps_ref.shape[0]
     reach = taps // 2
@@ -483,20 +549,15 @@
             conv = conv + padded[pl.ds(edge + start + t - reach, count)] * taps_ref[pl.ds(t, 1)].astype(F32)
         active[pl.ds(start, count)] = (conv * jax.nn.sigmoid(conv)).astype(BF16)
 
-    for start in range(tile, rows - tile, 32):
+    for start in range(0, rows, 32):
         convolve(start, 32)
-    await_bytes(halo, edge_sem)
-    padded[pl.ds(0, edge)] = jnp.where(lv > 0, halo[0, pl.ds(tile - edge, edge)].astype(F32), 0.0)
-    padded[pl.ds(edge + rows, edge)] = jnp.where(lv < groups - 1, halo[1, pl.ds(0, edge)].astype(F32), 0.0)
-    convolve(0, tile)
-    convolve(rows - tile, tile)
     mate_wait(JOIN)
-    after[...] += jnp.dot(active[...], weight(6, 0, width), preferred_element_type=F32)
+    after[inner] += jnp.dot(active[...], weight(6, 0, width), preferred_element_type=F32)
 
     @pl.loop(0, rows // chunk)
     def _(i):
         at = pl.ds(pl.multiple_of(i * chunk, chunk), chunk)
-        final[lv, at] = layer_norm(after[at]).astype(BF16)
+        final[lv, at] = layer_norm(after[pl.ds(pl.multiple_of(edge + i * chunk, 16), chunk)]).astype(BF16)
 
     def logits(block):
         at = pl.ds(pl.multiple_of(block * rows, rows), rows)
@@ -537,10 +598,8 @@
 
     for copy in sent[-SENDS:]:
         copy.wait_send()
-    await_send = make(
-        att_s.at[pl.ds(0, groups - 1)], att_s.at[pl.ds(0, groups - 1)], core_mate, att_send, recv_sem.at[0]
-    )
-    await_send.wait_send()
+    for i, ref in enumerate((att_s.at[pl.ds(0, groups - 1)],) + (att_s.at[pl.ds(0, groups - 1), pl.ds(0, edge)],) * 2):
+        make(ref, ref, core_mate, att_send.at[i], recv_sem.at[0]).wait_send()
 
 
 def body(
@@ -559,38 +618,33 @@
     frames = token_ids.shape[2]
     width = code_tables.shape[2]
     groups = lax.axis_size("level")
-    level = lax.axis_index("level")
     rows = frames // groups
-    done = levels_done[0]
-    use_token = (level < done) | (level == done) & (decoded_mask[0, 0] == 1)
-    sel = jnp.where(use_token, token_ids[0, 0], -1).astype(F32).reshape(groups, rows).T
     shard = w_project.shape[0]
-    tile, edge = 16, 8
+    wide = rows + 2 * EDGE
     vmem = pl.BlockSpec(memory_space=pltpu.VMEM)
     hbm = pl.BlockSpec(memory_space=pl.ANY)
     logits = pl.pallas_call(
         step_kernel,
         out_shape=pltpu.VMEM((frames, level_heads.shape[2]), BF16),
-        in_specs=[vmem] * 3 + [hbm] * 6,
+        in_specs=[vmem] * 2 + [pl.BlockSpec(memory_space=pltpu.SMEM)] + [vmem] * 2 + [hbm] * 6,
         out_specs=vmem,
         scratch_shapes=[
             pltpu.VMEM(code_tables.shape[1:], BF16),
             pltpu.VMEM(level_heads.shape[1:], BF16),
+            pltpu.VMEM((frames, LANES), F32),
             pltpu.VMEM((NZ * NY, NC, 7, shard, width), BF16),
             pltpu.VMEM((groups, rows, width), BF16),
             pltpu.VMEM((2, NX - 1, 2, rows, width // 2), BF16),
             pltpu.VMEM((2, rows, width // 2), BF16),
             pltpu.VMEM((2, rows, width // 2), BF16),
-            pltpu.VMEM((rows, width), F32),
-            pltpu.VMEM((rows, width), BF16),
+            pltpu.VMEM((wide, width), F32),
+            pltpu.VMEM((wide, width), BF16),
             pltpu.VMEM((groups, 3, rows, LANES), BF16),
             pltpu.VMEM((groups, 3, rows, LANES), BF16),
             pltpu.VMEM((groups, rows, LANES), BF16),
-            pltpu.VMEM((rows, width), BF16),
-            pltpu.VMEM((rows, width), F32),
-            pltpu.VMEM((rows, width), BF16),
-            pltpu.VMEM((2, tile, width), BF16),
-            pltpu.VMEM((rows + 2 * edge, width), F32),
+            pltpu.VMEM((wide, width), BF16),
+            pltpu.VMEM((wide, width), F32),
+            pltpu.VMEM((wide, width), F32),
             pltpu.VMEM((rows, width), BF16),
             pltpu.VMEM((groups, rows, width), BF16),
             pltpu.VMEM((groups, LANES * HEADS // width, rows, frames), BF16),
@@ -598,13 +652,15 @@
             pltpu.SemaphoreType.DMA((7,)),
             pltpu.SemaphoreType.DMA((SENDS,)),
             pltpu.SemaphoreType.DMA((ARRIVALS,)),
-            pltpu.SemaphoreType.DMA,
+            pltpu.SemaphoreType.DMA((3,)),
         ],
         compiler_params=pltpu.CompilerParams(
             collective_id=0, has_side_effects=True, vmem_limit_bytes=60 * 1024 * 1024
         ),
     )(
-        sel,
+        token_ids[0],
+        decoded_mask[0],
+        levels_done,
         mask_vectors,
         w_depth,
         code_tables[0],

time: 118 us -> 112 us (0.949)
  Pallas kernels: 113 us -> 110 us
    pallas_call x1, Pallas kernels: 113 us -> 110 us  [body(): pl.pallas_call(step_kernel, out_shape=pltpu.VMEM((frames, level_heads.sha...]
where the time goes in v4:
time: 112 us
  Pallas kernels  110 us (98%)
  local copies, waits for them, and re-layouts  1.67 us (1%)
    pallas_call x1, Pallas kernels, body(): pl.pallas_call(step_kernel, out_shape=pltpu.VMEM((frames, level_heads.sha...  110 us

profile of v4, /device:TPU:32, one launch (start us, length us, event | category | flops | bytes accessed | tf_op | source)
XLA Modules:
  0.0 112.0 jit_solution(14224784168704834650)
XLA Ops:
  0.7 109.7 %shard_map.109 = bf16[1536,1024]{1,0:T(8,128)(2,1)S(1)} custom-call(s32[1,1536]{1,0:T(1,128)} %bitcast.10, s32[1,1536]{1,0:T(1,128)} %bitcast.11, s32[1]{0:T(128)S(6)} %copy.14.done_ref, bf16[1,1024]{1,0:T(2,128)(2,1)} %fill_ref.1, bf16[5,1024]{1,0:T(8,128)(2,1)} %taps_ref.1, bf16[1024,1024]{1,0:T(8,128)(2,1)} %bitcast.7, bf16[3,32,128]{2,1,0:T(8,128)(2,1)} %wqkv_hbm.1, ...), custom_call_target="tpu_custom_call" | custom-call | tf_op jit(solution)/shard_map/pallas_call | solution.py:626
  110.4 1.7 %copy.13 = bf16[1,1,1536,1024]{3,2,1,0:T(8,128)(2,1)} copy(bf16[1,1,1536,1024]{3,2,1,0:T(8,128)(2,1)S(1)} %bitcast.6) | data formatting | bytes 6291456

commit v5 on v4

--- a/solution.py
+++ b/solution.py
@@ -13,7 +13,7 @@
 NX, NL = 4, 2
 LANES = 128
 EDGE = 16
-SENDS, ARRIVALS = 40, 104
+SENDS, ARRIVALS = 56, 106
 Q, K, V, OUT, EXPAND, JOIN = range(6)
 
 
@@ -293,10 +293,12 @@
         term(2 + 2 * (i // 2), lax.rem(i + 1, 2))
 
     columns_wait(0, 3, qkv_columns)
-    for g in (K, Q, V):
+    for g in (K, Q):
         z_start(g)
         y_start(g, 0)
     z_start(JOIN)
+    z_start(V)
+    y_start(V, 0)
     ring_next(1, 0)
     ring_send(1, 2)
     y_forward(K, 0)
@@ -311,16 +313,15 @@
     y_start(Q, 1)
     ring_next(2, 0)
     ring_next(1, 1)
+    z_forward(JOIN)
+    y_start(JOIN, -1)
+    y_start(JOIN, 1)
     z_forward(V)
     y_start(V, -1)
     y_start(V, 1)
-    z_forward(JOIN)
-    y_start(JOIN, -1)
-    y_start(JOIN, 1)
     ring_next(1, 2)
     columns_wait(3, 1, out_columns)
     z_start(OUT)
-    z_start(EXPAND)
     mate_start(K, 0)
     mate_start(Q, 0)
     mate_start(V, 0)
@@ -330,25 +331,26 @@
     y_start(Q, 2)
     y_forward(K, -1)
     y_forward(K, 1)
+    z_last(JOIN)
+    y_start(JOIN, 2)
     z_last(V)
     y_start(V, 2)
-    z_last(JOIN)
-    y_start(JOIN, 2)
     ring_next(3, 0)
+    z_start(EXPAND)
     ring_next(2, 1)
     y_forward(Q, -1)
     y_forward(Q, 1)
     ring_next(2, 2)
     z_forward(OUT)
+    y_forward(JOIN, -1)
+    y_forward(JOIN, 1)
     y_forward(V, -1)
     y_forward(V, 1)
-    y_forward(JOIN, -1)
-    y_forward(JOIN, 1)
     y_forward(K, 2)
     y_forward(Q, 2)
     ring_next(3, 1)
+    y_forward(JOIN, 2)
     y_forward(V, 2)
-    y_forward(JOIN, 2)
     for dz in (0, -1, 1):
         y_start(OUT, dz)
     y_forward(EXPAND, 0)
@@ -363,9 +365,6 @@
     mate_start(K, 2)
     mate_start(Q, 2)
     mate_start(V, 2)
-    z_forward(EXPAND)
-    y_start(EXPAND, -1)
-    y_start(EXPAND, 1)
     await_bytes(zrecv, z_sem)
     for d in range(2):
         own[inner, col(d)] += zrecv[d].astype(F32)
@@ -402,6 +401,9 @@
     k_sem = arrival()
     project(1)
     exchange(1, (k_sem,))
+    z_forward(EXPAND)
+    y_start(EXPAND, -1)
+    y_start(EXPAND, 1)
     mate_wait(Q)
     project(0)
     q_base = len(arrivals)
@@ -416,14 +418,8 @@
     send(own.at[pl.ds(edge, edge)], own.at[pl.ds(edge + rows, edge)], {"level": side[1]}, edge_sem)
     z_last(OUT)
     y_start(OUT, 2)
-    x_forward()
     for dz in (0, -1, 1):
         y_forward(OUT, dz)
-    mate_start(EXPAND, 0)
-    z_last(EXPAND)
-    y_start(EXPAND, 2)
-    y_forward(EXPAND, -1)
-    y_forward(EXPAND, 1)
     await_bytes(qkv_r.at[pl.ds(0, groups - 1), 1], k_sem)
 
     head_dim = width // HEADS
@@ -493,16 +489,22 @@
 
     score(0)
     scores_of(1, 3)
+    x_forward()
+    mate_start(EXPAND, 0)
     y_forward(OUT, 2)
     mate_start(OUT, 0)
+    y_forward(EXPAND, -1)
+    y_forward(EXPAND, 1)
     scores_of(3, 5)
     mate_start(OUT, -1)
     mate_start(OUT, 1)
+    z_last(EXPAND)
+    y_start(EXPAND, 2)
     scores_of(5, groups)
-    y_forward(EXPAND, 2)
     await_bytes(qkv_r.at[pl.ds(0, groups - 1), 2], v_sem)
     mixes_of(1, 4)
     mate_start(OUT, 2)
+    y_forward(EXPAND, 2)
     mate_start(EXPAND, -1)
     mate_start(EXPAND, 1)
     x_mate()
@@ -549,52 +551,61 @@
             conv = conv + padded[pl.ds(edge + start + t - reach, count)] * taps_ref[pl.ds(t, 1)].astype(F32)
         active[pl.ds(start, count)] = (conv * jax.nn.sigmoid(conv)).astype(BF16)
 
-    for start in range(0, rows, 32):
-        convolve(start, 32)
     mate_wait(JOIN)
-    after[inner] += jnp.dot(active[...], weight(6, 0, width), preferred_element_type=F32)
-
-    @pl.loop(0, rows // chunk)
-    def _(i):
-        at = pl.ds(pl.multiple_of(i * chunk, chunk), chunk)
-        final[lv, at] = layer_norm(after[pl.ds(pl.multiple_of(edge + i * chunk, 16), chunk)]).astype(BF16)
-
-    def logits(block):
-        at = pl.ds(pl.multiple_of(block * rows, rows), rows)
+
+    part = rows // 2
+    share = part // 6 // EDGE * EDGE
+    side_sems, mate_sems, far_sems, last_sems, tail_sems, cross_sems = ([arrival(), arrival()] for _ in range(6))
+
+    for n in range(2):
+        at, wide_at = pl.ds(n * part, part), pl.ds(edge + n * part, part)
+        for start in range(n * part, (n + 1) * part, 32):
+            convolve(start, 32)
+        after[wide_at] += jnp.dot(active[at], weight(6, 0, width), preferred_element_type=F32)
+        final[lv, at] = layer_norm(after[wide_at]).astype(BF16)
+        mine = final.at[lv, at]
+        send(mine, mine, x_up, side_sems[n])
+        send(mine, mine, x_down, side_sems[n])
+        send(mine, mine, z_mate, mate_sems[n])
+
+    def logits(block, start=0, count=rows):
+        at = pl.ds(pl.multiple_of(block * rows + start, 32), count)
+        states = final[block, pl.ds(start, count)]
         for h in range(2):
-            product = jnp.dot(final[block], head[:, col(h)], preferred_element_type=F32)
+            product = jnp.dot(states, head[:, col(h)], preferred_element_type=F32)
             out[at, col(h)] = product.astype(BF16)
 
-    mine = final.at[lv]
-    side_sem, mate_sem, far_sem, last_sem = arrival(), arrival(), arrival(), arrival()
-    down_sem, up_sem = arrival(), arrival()
-    send(mine, mine, x_up, side_sem)
-    send(mine, mine, x_down, side_sem)
-    send(mine, mine, z_mate, mate_sem)
-    top, bottom = pl.ds(0, rows // 2), pl.ds(rows // 2, rows // 2)
     loads[6].wait()
     logits(lv)
-    await_bytes(final.at[pl.ds(0, 2)], side_sem)
-    one, two = final.at[level_of(-1, 0), top], final.at[level_of(1, 0), bottom]
-    send(one, one, x_up, far_sem)
-    send(two, two, x_down, far_sem)
-    await_bytes(final.at[0], mate_sem)
-    mate_block = final.at[level_of(0, 1)]
-    send(mate_block, mate_block, x_up, down_sem)
-    send(mate_block, mate_block, x_down, up_sem)
+    for n in range(2):
+        start, middle = n * part, n * part + part // 2
+        await_bytes(final.at[pl.ds(0, 2), pl.ds(0, part)], side_sems[n])
+        one = final.at[level_of(-1, 0), pl.ds(start, part // 2)]
+        two = final.at[level_of(1, 0), pl.ds(middle, part // 2)]
+        send(one, one, x_up, far_sems[n])
+        send(two, two, x_down, far_sems[n])
+        for dx in (-1, 1):
+            tail = final.at[level_of(dx, 0), pl.ds(start + part - share, share)]
+            send(tail, tail, z_mate, tail_sems[n])
+    for n in range(2):
+        await_bytes(final.at[0, pl.ds(0, part)], mate_sems[n])
+        block = final.at[level_of(0, 1), pl.ds(n * part, part - share)]
+        send(block, block, x_up, cross_sems[n])
+        send(block, block, x_down, cross_sems[n])
     logits(level_of(-1, 0))
     logits(level_of(1, 0))
-    await_bytes(final.at[0], far_sem)
-    opposite = final.at[level_of(2, 0)]
-    send(opposite, opposite, z_mate, last_sem)
-    logits(level_of(0, 1))
-    logits(level_of(2, 0))
-    await_bytes(final.at[0], down_sem)
-    logits(level_of(-1, 1))
-    await_bytes(final.at[0], up_sem)
-    logits(level_of(1, 1))
-    await_bytes(final.at[0], last_sem)
-    logits(level_of(2, 1))
+    for n in range(2):
+        await_bytes(final.at[0, pl.ds(0, part)], far_sems[n])
+        block = final.at[level_of(2, 0), pl.ds(n * part, part)]
+        send(block, block, z_mate, last_sems[n])
+        logits(level_of(2 * n, 1 - n))
+    for n in range(2):
+        await_bytes(final.at[pl.ds(0, 2), pl.ds(0, part - share)], cross_sems[n])
+        await_bytes(final.at[pl.ds(0, 2), pl.ds(0, share)], tail_sems[n])
+        logits(level_of(-1, 1), n * part, part)
+        logits(level_of(1, 1), n * part, part)
+        await_bytes(final.at[0, pl.ds(0, part)], last_sems[n])
+        logits(level_of(2, 1), n * part, part)
 
     for copy in sent[-SENDS:]:
         copy.wait_send()

time: 112 us -> 108 us (0.964)
  Pallas kernels: 110 us -> 105 us
    pallas_call x1, Pallas kernels: 110 us -> 105 us  [body(): pl.pallas_call(step_kernel, out_shape=pltpu.VMEM((frames, level_heads.sha...]
where the time goes in v5:
time: 108 us
  Pallas kernels  105 us (97%)
  local copies, waits for them, and re-layouts  1.67 us (2%)
    pallas_call x1, Pallas kernels, body(): pl.pallas_call(step_kernel, out_shape=pltpu.VMEM((frames, level_heads.sha...  105 us

profile of v5, /device:TPU:32, one launch (start us, length us, event | category | flops | bytes accessed | tf_op | source)
XLA Modules:
  0.0 107.8 jit_solution(13830281900136984148)
XLA Ops:
  0.7 105.5 %shard_map.109 = bf16[1536,1024]{1,0:T(8,128)(2,1)S(1)} custom-call(s32[1,1536]{1,0:T(1,128)} %bitcast.10, s32[1,1536]{1,0:T(1,128)} %bitcast.11, s32[1]{0:T(128)S(6)} %copy.14.done_ref, bf16[1,1024]{1,0:T(2,128)(2,1)} %fill_ref.1, bf16[5,1024]{1,0:T(8,128)(2,1)} %taps_ref.1, bf16[1024,1024]{1,0:T(8,128)(2,1)} %bitcast.7, bf16[3,32,128]{2,1,0:T(8,128)(2,1)} %wqkv_hbm.1, ...), custom_call_target="tpu_custom_call" | custom-call | tf_op jit(solution)/shard_map/pallas_call | solution.py:637
  106.1 1.7 %copy.13 = bf16[1,1,1536,1024]{3,2,1,0:T(8,128)(2,1)} copy(bf16[1,1,1536,1024]{3,2,1,0:T(8,128)(2,1)S(1)} %bitcast.6) | data formatting | bytes 6291456

commit v6 on v5

--- a/solution.py
+++ b/solution.py
@@ -159,12 +159,6 @@
             send(block, partial.at[d, step - 1, 1 - dz, at], x_up if d == 0 else x_down, ring[step, p])
 
     ring = {}
-    loads[0].wait()
-
-    @pl.loop(0, 4)
-    def _(i):
-        term(2 * lax.rem(i, 2) + NX - 1, 1 - i // 2)
-
     spans = (pl.ds(0, 1), pl.ds(1, 1), pl.ds(2, 1), pl.ds(3, 1), pl.ds(4, 2), pl.ds(6, 1))
     low, high = pl.ds(0, shard // 2), pl.ds(shard // 2, shard // 2)
 
@@ -282,16 +276,20 @@
         await_bytes(weights.at[zy, core, pl.ds(j, count), :, pl.ds(0, (groups - 1) * LANES)], sem)
 
     qkv_columns = columns_start(0, 3)
+    y_start(EXPAND, 0)
+    y_start(JOIN, 0)
+    loads[0].wait()
+
+    def first_terms(first, last):
+        @pl.loop(first, last)
+        def _(i):
+            term(2 * lax.rem(i, 2) + NX - 1, 1 - i // 2)
+
+    first_terms(0, 2)
     ring_send(1, 0)
     out_columns = columns_start(3, 1)
+    first_terms(2, 4)
     ring_send(1, 1)
-    y_start(EXPAND, 0)
-    y_start(JOIN, 0)
-
-    @pl.loop(0, 4)
-    def _(i):
-        term(2 + 2 * (i // 2), lax.rem(i + 1, 2))
-
     columns_wait(0, 3, qkv_columns)
     for g in (K, Q):
         z_start(g)
@@ -299,6 +297,11 @@
     z_start(JOIN)
     z_start(V)
     y_start(V, 0)
+
+    @pl.loop(0, 4)
+    def _(i):
+        term(2 + 2 * (i // 2), lax.rem(i + 1, 2))
+
     ring_next(1, 0)
     ring_send(1, 2)
     y_forward(K, 0)
@@ -359,11 +362,11 @@
     mate_start(Q, -1)
     mate_start(Q, 1)
     ring_next(3, 2)
+    mate_start(K, 2)
+    mate_start(Q, 2)
     x_start()
     mate_start(V, -1)
     mate_start(V, 1)
-    mate_start(K, 2)
-    mate_start(Q, 2)
     mate_start(V, 2)
     await_bytes(zrecv, z_sem)
     for d in range(2):

time: 108 us -> 107 us (level)
  no operation moved by 1% of the time
where the time goes in v6:
time: 107 us
  Pallas kernels  105 us (98%)
  local copies, waits for them, and re-layouts  1.67 us (2%)
    pallas_call x1, Pallas kernels, body(): pl.pallas_call(step_kernel, out_shape=pltpu.VMEM((frames, level_heads.sha...  105 us

profile of v6, /device:TPU:32, one launch (start us, length us, event | category | flops | bytes accessed | tf_op | source)
XLA Modules:
  0.0 106.9 jit_solution(6144036248227034944)
XLA Ops:
  0.7 104.5 %shard_map.109 = bf16[1536,1024]{1,0:T(8,128)(2,1)S(1)} custom-call(s32[1,1536]{1,0:T(1,128)} %bitcast.10, s32[1,1536]{1,0:T(1,128)} %bitcast.11, s32[1]{0:T(128)S(6)} %copy.14.done_ref, bf16[1,1024]{1,0:T(2,128)(2,1)} %fill_ref.1, bf16[5,1024]{1,0:T(8,128)(2,1)} %taps_ref.1, bf16[1024,1024]{1,0:T(8,128)(2,1)} %bitcast.7, bf16[3,32,128]{2,1,0:T(8,128)(2,1)} %wqkv_hbm.1, ...), custom_call_target="tpu_custom_call" | custom-call | tf_op jit(solution)/shard_map/pallas_call | solution.py:640
  105.2 1.7 %copy.13 = bf16[1,1,1536,1024]{3,2,1,0:T(8,128)(2,1)} copy(bf16[1,1,1536,1024]{3,2,1,0:T(8,128)(2,1)S(1)} %bitcast.6) | data formatting | bytes 6291456
